TPU v7x, 256 devices: a whole 4x4x8 slice. The times are simulated.
256 devices in a mesh: fsdp: 32 (over z, x), rep: 8 (over y, core).
Axes of the slice: x: 4, y: 4, z: 8, core: 2. Of those that a mesh axis runs over, the one named last changes fastest.
Arguments:
- partials: bfloat16 [8, 112, 1024, 1024], P('rep', None, 'fsdp'), may hold values from -400 to 400
- sketch: bfloat16 [32, 8, 2, 1024, 256], P('fsdp', 'rep'), may hold values from -3 to 3
- owner_table: int32 [112, 1], replicated, may hold values from 0 to 31; in each aligned block of 14 rows (0 to 13, 14 to 27, ...) at most 2 rows name the same one
Outputs:
- update: bfloat16 [112, 1024, 1024], P('rep', 'fsdp')
- new_sketch: bfloat16 [32, 8, 2, 1024, 256], P('fsdp', 'rep')
Inputs may be any that keep to these rules, and one draw needn't show every extreme that they name: `owner_table`: in each aligned slice of 14 blocks no owner holds more than 2 blocks; some owner holds exactly 2 in some slice.
All inputs are finite; a program needn't handle non-finite values.
Results may differ from a plain program's by a relative error of at most 0.015.
Values may be sent and summed in bfloat16 or wider, within the bound.
A program may use at most 128 MiB of HBM per device.

v0:
```python
import functools
import math

import jax
import jax.numpy as jnp
from jax import lax
from jax.sharding import Mesh
from jax.sharding import PartitionSpec as P

NS_ITERS = 5
FSDP = ("fsdp_0", "fsdp_1")
REP = ("rep_0", "rep_1")
FSDP_REP = ("fsdp_0", "fsdp_1", "rep_0", "rep_1")


DECAY = 0.9
DAMPING = 64.0
FIRST_AXES = (((0,), (0,)), ((), ()))
LAST_AXES = (((1,), (1,)), ((), ()))


def one_axis_at_a_time(value, axes):
    return functools.reduce(lax.psum, axes, value)


def inverse_root(matrix, epsilon):
    identity = jnp.eye(matrix.shape[0], dtype=jnp.float32)
    trace_sum = jnp.trace(matrix) + epsilon
    current = matrix / trace_sum
    inverse = identity
    for repeat in range(NS_ITERS):
        middle = 1.5 * identity - 0.5 * jnp.dot(inverse, current, precision=lax.Precision.HIGHEST)
        current = jnp.dot(current, middle, precision=lax.Precision.HIGHEST)
        inverse = jnp.dot(middle, inverse, precision=lax.Precision.HIGHEST)
    return inverse / jnp.sqrt(trace_sum)


def precondition(gradient, current_sketch):
    identity = jnp.eye(current_sketch.shape[1], dtype=jnp.float32)
    projected = lax.dot_general(
        gradient, current_sketch, FIRST_AXES, preferred_element_type=jnp.float32
    ).astype(jnp.bfloat16)
    gram_matrix = lax.dot_general(
        current_sketch, current_sketch, FIRST_AXES, preferred_element_type=jnp.float32
    ).astype(jnp.bfloat16)
    powered = DECAY * jnp.dot(
        current_sketch, gram_matrix, preferred_element_type=jnp.float32
    ) + jnp.dot(gradient, projected, preferred_element_type=jnp.float32)
    inner_gram = lax.dot_general(powered, powered, FIRST_AXES, precision=lax.Precision.HIGHEST)
    basis_full = jnp.dot(powered, inverse_root(inner_gram, 1e-06), precision=lax.Precision.HIGHEST)
    basis_low = basis_full.astype(jnp.bfloat16)
    coefficients = lax.dot_general(
        gradient, basis_low, FIRST_AXES, preferred_element_type=jnp.float32
    ).astype(jnp.bfloat16)
    alignment = lax.dot_general(
        current_sketch, basis_low, FIRST_AXES, preferred_element_type=jnp.float32
    )
    energy = DECAY * lax.dot_general(
        alignment, alignment, FIRST_AXES, precision=lax.Precision.HIGHEST
    ) + lax.dot_general(coefficients, coefficients, FIRST_AXES, preferred_element_type=jnp.float32)
    root_inverse = inverse_root(energy + DAMPING * identity, 0.0)
    inner_part = jnp.dot(energy, root_inverse, precision=lax.Precision.HIGHEST)
    new_block = jnp.dot(basis_full, inner_part, precision=lax.Precision.HIGHEST).astype(
        jnp.bfloat16
    )
    mix_matrix = math.sqrt(DAMPING) * root_inverse - identity
    side_terms = lax.dot_general(
        coefficients.astype(jnp.float32), mix_matrix, LAST_AXES, precision=lax.Precision.HIGHEST
    ).astype(jnp.bfloat16)
    update_block = (
        gradient.astype(jnp.float32)
        + lax.dot_general(basis_low, side_terms, LAST_AXES, preferred_element_type=jnp.float32)
    ).astype(jnp.bfloat16)
    return (update_block, new_block)


def squared_sum(values):
    wide = values.astype(jnp.float32)
    return jnp.sum(wide * wide)


def process_slot(slot_index, arrived, clip_factor, held_sketches, filled):
    block_width = arrived.shape[-1]
    gradient = (clip_factor * arrived.reshape(block_width, block_width).astype(jnp.float32)).astype(
        jnp.bfloat16
    )
    current_sketch = held_sketches[slot_index]
    active = slot_index < filled
    update_block, new_block = precondition(gradient, current_sketch)
    new_block = jnp.where(active, new_block, current_sketch)
    return (update_block, new_block)


def local(partials, sketch, owner_table):
    block_total = partials.shape[1]
    row_count = partials.shape[2]
    block_width = partials.shape[3]
    fsdp_count = lax.axis_size(FSDP)
    per_slice = block_total // lax.axis_size(REP)
    slot_count = sketch.shape[2]
    reduced = lax.psum_scatter(
        partials[0].astype(jnp.float32).astype(jnp.bfloat16), REP, scatter_dimension=0, tiled=True
    )
    my_owners = lax.dynamic_slice_in_dim(
        owner_table[:, 0], lax.axis_index(REP) * per_slice, per_slice
    )
    positions = jnp.arange(per_slice, dtype=jnp.int32)
    same_owner = (my_owners[:, None] == my_owners[None, :]) & (
        positions[:, None] < positions[None, :]
    )
    rank_in = jnp.sum(same_owner.astype(jnp.int32), axis=0)
    target = rank_in * fsdp_count + my_owners
    selector = (
        target[None, :] == jnp.arange(slot_count * fsdp_count, dtype=jnp.int32)[:, None]
    ).astype(jnp.bfloat16)
    flattened = reduced.reshape(per_slice, row_count * block_width)
    outgoing = jnp.dot(selector, flattened, preferred_element_type=jnp.float32).astype(jnp.bfloat16)
    outgoing = outgoing.reshape(slot_count, fsdp_count, row_count, block_width)
    sum_squares = one_axis_at_a_time(squared_sum(reduced), FSDP_REP)
    clip_limit = 0.5 * math.sqrt(block_total * block_width * block_width)
    clip_factor = jnp.minimum(1.0, clip_limit / jnp.sqrt(sum_squares + 1e-06))
    filled = jnp.sum((my_owners == lax.axis_index(FSDP)).astype(jnp.int32))
    held_sketches = sketch[0, 0]
    fresh_list = []
    incoming = lax.all_to_all(outgoing, FSDP, split_axis=1, concat_axis=1, tiled=True)
    update_list = []
    for slot_index in range(slot_count):
        update_block, new_block = process_slot(
            slot_index, incoming[slot_index], clip_factor, held_sketches, filled
        )
        update_list.append(update_block)
        fresh_list.append(new_block)
    stacked = jnp.stack(update_list).reshape(slot_count, fsdp_count, row_count, block_width)
    returned = lax.all_to_all(stacked, FSDP, split_axis=1, concat_axis=1, tiled=True)
    returned = returned.reshape(slot_count * fsdp_count, row_count * block_width)
    my_updates = lax.dot_general(
        selector, returned, FIRST_AXES, preferred_element_type=jnp.float32
    ).astype(jnp.bfloat16)
    my_updates = my_updates.reshape(per_slice, row_count, block_width)
    return (my_updates, jnp.stack(fresh_list)[None, None])


def solution(mesh):
    torus = Mesh(mesh.devices.reshape(8, 4, 4, 2), ("fsdp_0", "fsdp_1", "rep_0", "rep_1"))
    return jax.shard_map(
        local,
        mesh=torus,
        in_specs=(P(REP, None, FSDP, None), P(FSDP, REP, None, None, None), P()),
        out_specs=(P(REP, FSDP, None), P(FSDP, REP, None, None, None)),
        check_vma=False,
    )
```

profile of v0, /device:TPU:2, one launch (start us, length us, event | category | flops | bytes accessed | tf_op | source)
XLA Modules:
  0.0 398.8 jit_solution(14725712927055801208)
XLA Ops:
  7.2 0.7 reduce-scatter.2.cloned.1.call-update
  7.9 0.8 fusion.55
  8.8 54.8 %reduce-scatter.2.cloned.1.call-done = bf16[14,32,1024]{2,1,0:T(8,128)(2,1)} async-done(((bf16[112,32,1024]{2,1,0:T(8,128)(2,1)}), bf16[14,32,1024]{2,1,0:T(8,128)(2,1)}) %reduce-scatter.2.cloned.1.call-update) | async-done | bytes 917520 | tf_op jit(solution)/shard_map/reduce_scatter | solution.py:101
  63.6 1.3 pad.4
  64.9 0.6 copy.26
  65.4 1.2 convolution_convert_fusion
  66.7 2.5 copy.27
  69.1 2.4 copy.18
  71.5 10.3 %all-to-all-start = ((bf16[2,32,32,1024]{3,2,0,1:T(8,128)(2,1)}), bf16[2,32,32,1024]{3,2,0,1:T(8,128)(2,1)}, u32[]{:S(2)}, u32[]{:S(2)}) async-start(bf16[2,32,32,1024]{3,2,0,1:T(8,128)(2,1)} %copy.18), calls=%async_computation.1 | async-start | bytes 8388608 | tf_op jit(solution)/shard_map/all_to_all | solution.py:125
  81.9 1.1 multiply_reduce_fusion
  83.0 101.3 %psum.28 = f32[]{:T(128)} all-reduce(f32[]{:T(128)} %multiply_reduce_fusion), channel_id=1, replica_groups=mesh['fsdp_0'=8,'fsdp_1'=4,'rep_0'=4,'rep_1'=2] {'fsdp_0'}, use_global_device_ids=true, to_apply=%region_3.0 | all-reduce | flops 1 | bytes 8 | tf_op jit(solution)/shard_map/psum | solution.py:23
  184.3 9.2 %psum.29 = f32[]{:T(128)} all-reduce(f32[]{:T(128)} %psum.28), channel_id=1, replica_groups=mesh['fsdp_0'=8,'fsdp_1'=4,'rep_0'=4,'rep_1'=2] {'fsdp_1'}, use_global_device_ids=true, to_apply=%region_4.0 | all-reduce | flops 1 | bytes 8 | tf_op jit(solution)/shard_map/psum | solution.py:23
  193.5 11.9 %psum.30 = f32[]{:T(128)} all-reduce(f32[]{:T(128)} %psum.29), channel_id=1, replica_groups=mesh['fsdp_0'=8,'fsdp_1'=4,'rep_0'=4,'rep_1'=2] {'rep_0'}, use_global_device_ids=true, to_apply=%region_5.0 | all-reduce | flops 1 | bytes 8 | tf_op jit(solution)/shard_map/psum | solution.py:23
  205.4 3.5 psum.31
  209.6 5.0 %multiply_convert_fusion.1 = (bf16[1,32,32,1024]{3,2,0,1:T(8,128)(2,1)}, bf16[1,32,32,1024]{3,2,0,1:T(8,128)(2,1)S(1)}) fusion(bf16[2,32,32,1024]{3,2,0,1:T(8,128)(2,1)} %all-to-all-done, f32[]{:T(128)S(6)} %min_shard_map.3), kind=kLoop, calls=%fused_computation.6 | loop fusion | flops 6291456 | bytes 8388612 | tf_op jit(solution)/shard_map/convert_element_type | solution.py:84
  214.6 1.3 copy-done.5
  216.0 3.2 fusion.11
  219.2 2.1 fusion.1
  221.3 1.6 select_reduce_fusion.1
  224.0 0.4 fusion.45
  225.8 0.4 select_subtract_fusion.7
  227.0 0.4 select_subtract_fusion.6
  228.1 0.4 select_subtract_fusion.5
  228.9 1.8 fusion.92
  231.1 1.0 convolution_convert_fusion.6
  232.1 0.8 copy-done.8
  233.2 1.0 select_reduce_fusion
  234.9 1.0 select_subtract_fusion.4
  235.9 1.0 fusion.46
  237.2 0.4 select_subtract_fusion.3
  238.4 0.4 select_subtract_fusion.2
  239.6 0.4 select_subtract_fusion.1
  240.3 1.1 fusion.99
  241.4 5.5 %fusion.10 = f32[1024,256]{0,1:T(8,128)} fusion(bf16[1024,1024]{1,0:T(8,128)(2,1)} %bitcast.194, bf16[1,1,2,1024,256]{4,3,2,1,0:T(8,128)(2,1)S(1)} %copy-done), kind=kOutput, calls=%fused_computation.76 | convolution fusion | flops 1074003968 | bytes 5767168 | tf_op jit(solution)/shard_map/dot_general | solution.py:48
  246.9 2.1 fusion.3
  249.0 2.3 select_reduce_fusion.3
  252.0 1.3 select_subtract_fusion.19
  253.3 1.3 fusion.44
  257.2 0.6 select_subtract_fusion.16
  259.4 1.8 fusion.78
  261.6 0.8 convolution_convert_fusion.8
  262.7 0.4 copy-done.10
  263.1 1.0 select_reduce_fusion.2
  264.9 1.0 select_subtract_fusion.14
  265.9 1.0 fusion.49
  270.7 0.4 select_subtract_fusion
  271.5 0.7 copy-done.14
  272.2 0.6 convolution_convert_fusion.4
  272.9 0.7 add_convert_fusion
  274.0 0.6 convolution_divide_fusion.2
  274.7 0.6 convolution_convert_fusion.5
  275.4 0.7 add_convert_fusion.1
  276.1 2.3 pad_maximum_fusion
  278.5 7.3 %all-to-all-start.1 = ((bf16[2,32,32,1024]{3,2,0,1:T(8,128)(2,1)}), bf16[2,32,32,1024]{3,2,0,1:T(8,128)(2,1)}, u32[]{:S(2)}, u32[]{:S(2)}) async-start(bf16[2,32,32,1024]{3,2,0,1:T(8,128)(2,1)} %pad_maximum_fusion), calls=%async_computation.2 | async-start | bytes 8388608 | tf_op jit(solution)/shard_map/all_to_all | solution.py:134
  287.1 1.4 fusion.101
  288.5 1.0 fusion.7
  289.9 1.0 fusion.5
  290.9 1.1 maximum_bitcast_fusion
  292.0 92.0 %all-to-all-done.1 = bf16[2,32,32,1024]{3,2,0,1:T(8,128)(2,1)} async-done(((bf16[2,32,32,1024]{3,2,0,1:T(8,128)(2,1)}), bf16[2,32,32,1024]{3,2,0,1:T(8,128)(2,1)}, u32[]{:S(2)}, u32[]{:S(2)}) %all-to-all-start.1) | async-done | bytes 4194336 | tf_op jit(solution)/shard_map/all_to_all | solution.py:134
  383.9 2.6 copy.23
  386.6 2.6 copy.28
  389.2 0.7 convolution_convert_fusion.1
  389.9 0.6 copy.29
  390.5 1.0 slice.20
  (88 shorter events, 16.3 us)
Async XLA Ops:
  7.2 56.4 %reduce-scatter.2.cloned.1.call-start = ((), (), s32[]{:S(2)}) async-start(), calls=%async_computation.3 | async-start | bytes 8257536 | tf_op jit(solution)/shard_map/reduce_scatter | solution.py:101
  7.2 0.7 copy-start.21
  71.5 10.3 %copy-start.12 = (bf16[14,32,1024]{2,1,0:T(8,128)(2,1)S(1)}, bf16[14,32,1024]{2,1,0:T(8,128)(2,1)}, u32[]{:S(2)}) copy-start(bf16[14,32,1024]{2,1,0:T(8,128)(2,1)} %reduce-scatter.2.cloned.1.call-done) | copy-start | bytes 2752516
  71.5 138.1 %all-to-all-start = ((bf16[2,32,32,1024]{3,2,0,1:T(8,128)(2,1)}), bf16[2,32,32,1024]{3,2,0,1:T(8,128)(2,1)}, u32[]{:S(2)}, u32[]{:S(2)}) async-start(bf16[2,32,32,1024]{3,2,0,1:T(8,128)(2,1)} %copy.18), calls=%async_computation.1 | async-start | bytes 8388608 | tf_op jit(solution)/shard_map/all_to_all | solution.py:125
  209.6 6.4 %copy-start = (bf16[1,1,2,1024,256]{4,3,2,1,0:T(8,128)(2,1)S(1)}, bf16[1,1,2,1024,256]{4,3,2,1,0:T(8,128)(2,1)}, u32[]{:S(2)}) copy-start(bf16[1,1,2,1024,256]{4,3,2,1,0:T(8,128)(2,1)} %param.4) | copy-start | bytes 3145732
  214.6 1.4 copy-start.5
  228.9 2.2 copy-start.6
  232.1 0.8 copy-start.8
  234.2 3.8 copy-start.18
  259.4 2.2 copy-start.3
  261.2 1.1 copy-start.1
  262.3 0.8 copy-start.10
  264.2 3.8 copy-start.19
  268.7 2.0 copy-start.13
  269.5 2.7 copy-start.9
  270.3 2.6 copy-start.7
  271.5 0.7 copy-start.14
  272.9 1.8 copy-start.11
  272.9 2.5 copy-start.4
  273.6 1.7 copy-start.2
  274.7 1.4 copy-start.16
  278.5 8.7 %copy-start.15 = (f32[256,256]{1,0:T(8,128)S(1)}, f32[256,256]{1,0:T(8,128)}, u32[]{:S(2)}) copy-start(f32[256,256]{1,0:T(8,128)} %copy-done.14) | copy-start | bytes 786436
  278.5 105.5 %all-to-all-start.1 = ((bf16[2,32,32,1024]{3,2,0,1:T(8,128)(2,1)}), bf16[2,32,32,1024]{3,2,0,1:T(8,128)(2,1)}, u32[]{:S(2)}, u32[]{:S(2)}) async-start(bf16[2,32,32,1024]{3,2,0,1:T(8,128)(2,1)} %pad_maximum_fusion), calls=%async_computation.2 | async-start | bytes 8388608 | tf_op jit(solution)/shard_map/all_to_all | solution.py:134
  287.1 2.4 copy-start.17
  287.1 2.4 copy-start.20
Sparse Core Ops, SparseCore 0:
  10.5 52.9 reduce-scatter.1
where the time goes:
time: 404 us; the launch traced here: 399 us
  waiting for transfers between devices  147 us (36%)
  blocking collectives  126 us (31%)
  matrix products  60.3 us (15%)
  between operations  20.2 us (5%)
  starting transfers between devices  17.6 us (4%)
  local copies, waits for them, and re-layouts  17 us (4%)
  other arithmetic  10.3 us (3%)
    psum x4, blocking collectives, one_axis_at_a_time(): return functools.reduce(lax.psum, axes, value)  126 us
    all_to_all x1, waiting for transfers between devices, local(): lax.all_to_all(stacked, FSDP, split_axis=1, concat_axis=1, tiled=True)  92 us
    reduce_scatter x1, waiting for transfers between devices, local(): lax.psum_scatter(partials[0].astype(jnp.float32).astype(jnp.bfloat16), RE...  54.8 us
    unnamed x49, local copies, waits for them, and re-layouts  10.9 us
    all_to_all x1, starting transfers between devices, local(): lax.all_to_all(outgoing, FSDP, split_axis=1, concat_axis=1, tiled=True)  10.3 us
    dot_general x20, matrix products, inverse_root(): jnp.dot(inverse, current, precision=lax.Precision.HIGHEST)  9.84 us
    dot_general x16, matrix products, inverse_root(): current = jnp.dot(current, middle, precision=lax.Precision.HIGHEST)  9.04 us
    dot_general x2, matrix products, precondition(): jnp.dot(gradient, projected, preferred_element_type=jnp.float32)  8.72 us
  transfers between devices with their start and end apart: 3, of which 2 were waited for; matrix products, arithmetic and copies ran while one was open for 2% of the time, Pallas kernels for 0%

commit v1 on v0

v1 whole, which is shorter than its diff:
```python
import functools
import math

import jax
import jax.numpy as jnp
from jax import lax
from jax.experimental import pallas as pl
from jax.experimental.pallas import tpu as pltpu
from jax.sharding import PartitionSpec as P

NS_ITERS = 5
DECAY = 0.9
DAMPING = 64.0
FIRST_AXES = (((0,), (0,)), ((), ()))
LAST_AXES = (((1,), (1,)), ((), ()))
MESH = pl.DeviceIdType.MESH
F32 = jnp.float32
BF16 = jnp.bfloat16


def inverse_root(matrix, epsilon):
    identity = jnp.eye(matrix.shape[0], dtype=jnp.float32)
    trace_sum = jnp.trace(matrix) + epsilon
    current = matrix / trace_sum
    inverse = identity
    for repeat in range(NS_ITERS):
        middle = 1.5 * identity - 0.5 * jnp.dot(inverse, current, precision=lax.Precision.HIGHEST)
        current = jnp.dot(current, middle, precision=lax.Precision.HIGHEST)
        inverse = jnp.dot(middle, inverse, precision=lax.Precision.HIGHEST)
    return inverse / jnp.sqrt(trace_sum)


def precondition(gradient, current_sketch):
    identity = jnp.eye(current_sketch.shape[1], dtype=jnp.float32)
    projected = lax.dot_general(
        gradient, current_sketch, FIRST_AXES, preferred_element_type=jnp.float32
    ).astype(jnp.bfloat16)
    gram_matrix = lax.dot_general(
        current_sketch, current_sketch, FIRST_AXES, preferred_element_type=jnp.float32
    ).astype(jnp.bfloat16)
    powered = DECAY * jnp.dot(
        current_sketch, gram_matrix, preferred_element_type=jnp.float32
    ) + jnp.dot(gradient, projected, preferred_element_type=jnp.float32)
    inner_gram = lax.dot_general(powered, powered, FIRST_AXES, precision=lax.Precision.HIGHEST)
    basis_full = jnp.dot(powered, inverse_root(inner_gram, 1e-06), precision=lax.Precision.HIGHEST)
    basis_low = basis_full.astype(jnp.bfloat16)
    coefficients = lax.dot_general(
        gradient, basis_low, FIRST_AXES, preferred_element_type=jnp.float32
    ).astype(jnp.bfloat16)
    alignment = lax.dot_general(
        current_sketch, basis_low, FIRST_AXES, preferred_element_type=jnp.float32
    )
    energy = DECAY * lax.dot_general(
        alignment, alignment, FIRST_AXES, precision=lax.Precision.HIGHEST
    ) + lax.dot_general(coefficients, coefficients, FIRST_AXES, preferred_element_type=jnp.float32)
    root_inverse = inverse_root(energy + DAMPING * identity, 0.0)
    inner_part = jnp.dot(energy, root_inverse, precision=lax.Precision.HIGHEST)
    new_block = jnp.dot(basis_full, inner_part, precision=lax.Precision.HIGHEST).astype(
        jnp.bfloat16
    )
    mix_matrix = math.sqrt(DAMPING) * root_inverse - identity
    side_terms = lax.dot_general(
        coefficients.astype(jnp.float32), mix_matrix, LAST_AXES, precision=lax.Precision.HIGHEST
    ).astype(jnp.bfloat16)
    update_block = (
        gradient.astype(jnp.float32)
        + lax.dot_general(basis_low, side_terms, LAST_AXES, preferred_element_type=jnp.float32)
    ).astype(jnp.bfloat16)
    return (update_block, new_block)


def wait_bytes(ref, sem):
    pltpu.make_async_copy(ref, ref, sem).wait()


def put(src, dst, send, recv, device):
    pltpu.make_async_remote_copy(
        src_ref=src, dst_ref=dst, send_sem=send, recv_sem=recv, device_id=device, device_id_type=MESH
    ).start()


def barrier_with(f, r, nf, nr, with_rep):
    barrier = pltpu.get_barrier_semaphore()

    def to_fsdp(i, carry):
        pl.semaphore_signal(barrier, inc=1, device_id=(lax.rem(f + i, nf), r), device_id_type=MESH)
        return carry

    def to_rep(i, carry):
        pl.semaphore_signal(barrier, inc=1, device_id=(f, lax.rem(r + i, nr)), device_id_type=MESH)
        return carry

    lax.fori_loop(1, nf, to_fsdp, 0)
    if with_rep:
        lax.fori_loop(1, nr, to_rep, 0)
    pl.semaphore_wait(barrier, nf - 1 + (nr - 1 if with_rep else 0))


def gather_kernel(
    nf, nr, slot_ref, part, sk, g_out, z_out, ss_out,
    own, rc, s_a, r_a, s_b, r_b, fin, sk_r, sk_s, ss_a, ss_b,
    own_sem, rc_sem, ra_sem, rb_sem, gz_sem, send_sem,
):
    f = lax.axis_index("fsdp")
    r = lax.axis_index("rep")
    ny = nr // 2
    steps = own.shape[2]
    rows = own.shape[3]
    y = r // 2
    c = lax.rem(r, 2)
    partner = (f, 2 * y + 1 - c)
    ydev = ((f, 2 * lax.rem(y + 1, ny) + c), (f, 2 * lax.rem(y + ny - 1, ny) + c))
    rel = (1, ny - 1)

    for d in (2, 1, 3, 0):
        pltpu.make_async_copy(part.at[2 * lax.rem(y + d, ny) + c], own.at[d], own_sem.at[d]).start()

    barrier_with(f, r, nf, nr, True)

    for k in range(steps):
        for d in (2, 1, 3, 0):
            put(part.at[2 * lax.rem(y + d, ny) + 1 - c, :, k], rc.at[d, :, k], send_sem.at[0], rc_sem.at[d, k], partner)
        if k == 0:
            def spread(i, carry):
                t = lax.rem(f + i, nf)
                put(sk.at[:, pl.ds(pl.multiple_of(t * rows, rows), rows), :], sk_r.at[f], send_sem.at[1], gz_sem.at[0], (t, r))
                return carry

            lax.fori_loop(1, nf, spread, 0)
            mine = pltpu.make_async_copy(sk.at[:, pl.ds(pl.multiple_of(f * rows, rows), rows), :], sk_r.at[f], gz_sem.at[3])
            mine.start()

    for d in (2, 1, 3, 0):
        pltpu.make_async_copy(own.at[d], own.at[d], own_sem.at[d]).wait()

    def both(d, h, k):
        return own[d, h, k].astype(F32) + rc[d, h, k].astype(F32)

    def dependent(k):
        for d in (0, 1):
            wait_bytes(r_a.at[d, k], ra_sem.at[d, k])
            s_b[d, d, k] = (both(rel[d], d, k) + r_a[d, k].astype(F32)).astype(BF16)
            put(s_b.at[d, d, k], r_b.at[d, d, k], send_sem.at[3], rb_sem.at[d, d, k], ydev[d])

    def final(k, total):
        wait_bytes(rc.at[0, :, k], rc_sem.at[0, k])
        for h in (0, 1):
            wait_bytes(r_b.at[1 - h, h, k], rb_sem.at[1 - h, h, k])
            wait_bytes(r_b.at[h, h, k], rb_sem.at[h, h, k])
            value = (both(0, h, k) + (r_b[0, h, k].astype(F32) + r_b[1, h, k].astype(F32))).astype(BF16)
            fin[h, k] = value
            wide = value.astype(F32)
            square = wide * wide
            total = total + jnp.sum(square.reshape(rows // 8, 8, square.shape[1] // 128, 128).transpose(0, 2, 1, 3).reshape(-1, 8, 128), axis=0)
            target = 2 * (h * steps + k) + c

            @pl.when(target != f)
            def _():
                put(fin.at[h, k], g_out.at[f], send_sem.at[4], gz_sem.at[1], (target, r))

            @pl.when(target == f)
            def _():
                g_out[f] = value
        return total

    total = jnp.zeros((8, 128), F32)
    for k in range(steps):
        wait_bytes(rc.at[2, :, k], rc_sem.at[2, k])
        for d in (0, 1):
            s_a[d, k] = both(2, d, k).astype(BF16)
            put(s_a.at[d, k], r_a.at[d, k], send_sem.at[2], ra_sem.at[d, k], ydev[d])
        for d in (0, 1):
            wait_bytes(rc.at[rel[d], :, k], rc_sem.at[rel[d], k])
            s_b[d, 1 - d, k] = both(rel[d], 1 - d, k).astype(BF16)
            put(s_b.at[d, 1 - d, k], r_b.at[d, 1 - d, k], send_sem.at[3], rb_sem.at[d, 1 - d, k], ydev[d])
        if k >= 1:
            dependent(k - 1)
        if k >= 3:
            total = final(k - 3, total)
    dependent(steps - 1)
    for k in range(steps - 3, steps):
        total = final(k, total)

    ss_a[r] = total

    def rep_send(i, carry):
        put(ss_a.at[r], ss_a.at[r], send_sem.at[5], gz_sem.at[4], (f, lax.rem(r + i, nr)))
        return carry

    lax.fori_loop(1, nr, rep_send, 0)

    mine.wait()
    wait_bytes(sk_r.at[pl.ds(0, nf - 1)], gz_sem.at[0])
    for j in range(2 * steps):
        target = 2 * j + c
        slot = slot_ref[j]
        sk_s[j] = sk_r[slot // 2, lax.rem(slot, 2)]

        @pl.when(target != f)
        def _():
            put(sk_s.at[j], z_out.at[f], send_sem.at[6], gz_sem.at[2], (target, r))

        @pl.when(target == f)
        def _():
            z_out[f] = sk_s[j]

    wait_bytes(ss_a.at[pl.ds(0, nr - 1)], gz_sem.at[4])
    ss_b[f] = jnp.sum(ss_a[...], axis=0)

    def fsdp_send(i, carry):
        put(ss_b.at[f], ss_b.at[f], send_sem.at[7], gz_sem.at[5], (lax.rem(f + i, nf), r))
        return carry

    lax.fori_loop(1, nf, fsdp_send, 0)
    wait_bytes(ss_b.at[pl.ds(0, nf - 1)], gz_sem.at[5])
    ss_out[...] = jnp.sum(ss_b[...], axis=0)

    wait_bytes(rc, send_sem.at[0])
    wait_bytes(sk_r.at[pl.ds(0, nf - 1)], send_sem.at[1])
    wait_bytes(s_a, send_sem.at[2])
    wait_bytes(s_b, send_sem.at[3])
    wait_bytes(ss_a.at[pl.ds(0, nr - 1)], send_sem.at[5])
    wait_bytes(ss_b.at[pl.ds(0, nf - 1)], send_sem.at[7])
    busy = (lax.rem(f, 2) == c) & (f < 4 * steps)

    @pl.when(busy)
    def _():
        wait_bytes(g_out.at[pl.ds(0, 2 * steps - 1)], send_sem.at[4])
        wait_bytes(z_out.at[pl.ds(0, 2 * steps - 1)], send_sem.at[6])
        wait_bytes(g_out.at[pl.ds(0, nf - 1)], gz_sem.at[1])
        wait_bytes(z_out.at[pl.ds(0, nf - 1)], gz_sem.at[2])

    @pl.when(jnp.logical_not(busy))
    def _():
        wait_bytes(g_out.at[pl.ds(0, 2 * steps)], send_sem.at[4])
        wait_bytes(z_out.at[pl.ds(0, 2 * steps)], send_sem.at[6])


def scatter_kernel(
    nf, nr, back_ref, up, new, upd_out, nk_out, s_r, s_x, recv_sem, send_sem,
):
    f = lax.axis_index("fsdp")
    r = lax.axis_index("rep")
    c = lax.rem(r, 2)
    blocks = upd_out.shape[0]
    rows = upd_out.shape[1]
    busy = (lax.rem(f, 2) == c) & (f < 2 * blocks)
    j = f // 2
    barrier_with(f, r, nf, nr, False)

    @pl.when(busy)
    def _():
        def send_new(i, carry):
            t = lax.rem(f + i, nf)
            put(new.at[t], s_r.at[j], send_sem.at[0], recv_sem.at[0], (t, r))
            return carry

        def send_up(i, carry):
            t = lax.rem(f + i, nf)
            put(up.at[t], upd_out.at[j], send_sem.at[1], recv_sem.at[1], (t, r))
            return carry

        lax.fori_loop(1, nf, send_new, 0)
        lax.fori_loop(1, nf, send_up, 0)
        s_r[j] = new[f]
        upd_out[j] = up[f]
        wait_bytes(s_r.at[pl.ds(0, blocks - 1)], recv_sem.at[0])

    @pl.when(jnp.logical_not(busy))
    def _():
        wait_bytes(s_r, recv_sem.at[0])

    def spread(i, carry):
        t = lax.rem(f + i, nf)
        for q in (0, 1):
            s_x[t, q] = s_r[back_ref[2 * t + q]]
        put(s_x.at[t], nk_out.at[f], send_sem.at[2], recv_sem.at[2], (t, r))
        return carry

    lax.fori_loop(1, nf, spread, 0)
    for q in (0, 1):
        nk_out[f, q] = s_r[back_ref[2 * f + q]]

    wait_bytes(nk_out.at[pl.ds(0, nf - 1)], recv_sem.at[2])
    wait_bytes(nk_out.at[pl.ds(0, nf - 1)], send_sem.at[2])

    @pl.when(busy)
    def _():
        wait_bytes(upd_out.at[pl.ds(0, blocks - 1)], recv_sem.at[1])
        wait_bytes(new.at[pl.ds(0, nf - 1)], send_sem.at[0])
        wait_bytes(up.at[pl.ds(0, nf - 1)], send_sem.at[1])

    @pl.when(jnp.logical_not(busy))
    def _():
        wait_bytes(upd_out, recv_sem.at[1])


def local(nf, nr, partials, sketch, owner_table):
    blocks_all, rows, width = partials.shape[1:]
    per_slice = blocks_all // nr
    half = per_slice // 2
    rank = sketch.shape[4]
    ny = nr // 2
    vmem = pl.BlockSpec(memory_space=pltpu.VMEM)
    anyw = pl.BlockSpec(memory_space=pl.ANY)
    smem = pl.BlockSpec(memory_space=pltpu.SMEM)
    dma = pltpu.SemaphoreType.DMA

    owners = lax.dynamic_slice_in_dim(owner_table[:, 0], lax.axis_index("rep") * per_slice, per_slice)
    position = jnp.arange(per_slice, dtype=jnp.int32)
    same = (owners[:, None] == owners[None, :]) & (position[:, None] < position[None, :])
    slots = owners * 2 + jnp.sum(same.astype(jnp.int32), axis=0)
    hit = slots[:, None] == jnp.arange(2 * nf, dtype=jnp.int32)[None, :]
    back = jnp.sum(jnp.where(hit, position[:, None], 0), axis=0)
    filled = jnp.sum((owners == lax.axis_index("fsdp")).astype(jnp.int32))

    part = partials.reshape(nr, 2, half, rows, width)
    held = sketch[0, 0]
    g_rows, z_rows, squares = pl.pallas_call(
        functools.partial(gather_kernel, nf, nr),
        out_shape=(
            jax.ShapeDtypeStruct((nf, rows, width), BF16),
            jax.ShapeDtypeStruct((nf, rows, rank), BF16),
            jax.ShapeDtypeStruct((8, 128), F32),
        ),
        in_specs=[smem, anyw, anyw],
        out_specs=(vmem, vmem, vmem),
        scratch_shapes=[
            pltpu.VMEM((ny, 2, half, rows, width), BF16),
            pltpu.VMEM((ny, 2, half, rows, width), BF16),
            pltpu.VMEM((2, half, rows, width), BF16),
            pltpu.VMEM((2, half, rows, width), BF16),
            pltpu.VMEM((2, 2, half, rows, width), BF16),
            pltpu.VMEM((2, 2, half, rows, width), BF16),
            pltpu.VMEM((2, half, rows, width), BF16),
            pltpu.VMEM((nf, 2, rows, rank), BF16),
            pltpu.VMEM((per_slice, rows, rank), BF16),
            pltpu.VMEM((nr, 8, 128), F32),
            pltpu.VMEM((nf, 8, 128), F32),
            dma((ny,)),
            dma((ny, half)),
            dma((2, half)),
            dma((2, 2, half)),
            dma((6,)),
            dma((8,)),
        ],
        compiler_params=pltpu.CompilerParams(collective_id=0, has_side_effects=True),
    )(slots, part, held)

    size = blocks_all * width * width
    sum_squares = jnp.sum(squares)
    clip_factor = jnp.minimum(1.0, 0.5 * math.sqrt(size) / jnp.sqrt(sum_squares + 1e-06))
    gradient = (clip_factor * g_rows.reshape(width, width).astype(F32)).astype(BF16)
    update_block, new_block = precondition(gradient, z_rows.reshape(width, rank))

    upd, fresh = pl.pallas_call(
        functools.partial(scatter_kernel, nf, nr),
        out_shape=(
            jax.ShapeDtypeStruct((per_slice, rows, width), BF16),
            jax.ShapeDtypeStruct((nf, 2, rows, rank), BF16),
        ),
        in_specs=[smem, vmem, vmem],
        out_specs=(vmem, vmem),
        scratch_shapes=[
            pltpu.VMEM((per_slice, rows, rank), BF16),
            pltpu.VMEM((nf, 2, rows, rank), BF16),
            dma((3,)),
            dma((3,)),
        ],
        compiler_params=pltpu.CompilerParams(collective_id=1, has_side_effects=True),
    )(back, update_block.reshape(nf, rows, width), new_block.reshape(nf, rows, rank))
    fresh = fresh.transpose(1, 0, 2, 3).reshape(2, nf * rows, rank)
    keep = jnp.arange(2, dtype=jnp.int32)[:, None, None] < filled
    return upd, jnp.where(keep, fresh, held)[None, None]


def solution(mesh):
    nf, nr = mesh.shape["fsdp"], mesh.shape["rep"]
    return jax.shard_map(
        functools.partial(local, nf, nr),
        mesh=mesh,
        in_specs=(P("rep", None, "fsdp", None), P("fsdp", "rep", None, None, None), P()),
        out_specs=(P("rep", "fsdp", None), P("fsdp", "rep", None, None, None)),
        check_vma=False,
    )
```

time: 404 us -> 177 us (0.44); the launches traced: 399 us -> 176 us
  waiting for transfers between devices: 147 us -> 0 us
  Pallas kernels: 0 us -> 132 us
  blocking collectives: 126 us -> 0 us
  matrix products: 60.3 us -> 28.1 us
  starting transfers between devices: 17.6 us -> 0 us
  between operations: 20.2 us -> 3.09 us
  local copies, waits for them, and re-layouts: 17 us -> 3.84 us
    pallas_call x0 -> x2, Pallas kernels: none -> 132 us  [the longest x1 71.2 us: local(): pl.pallas_call(functools.partial(gather_kernel, nf, nr), out_shape=(jax.S...]
    psum x4 -> x0, blocking collectives: 126 us -> none  [one_axis_at_a_time(): return functools.reduce(lax.psum, axes, value)]
    all_to_all x2 -> x0, waiting for transfers between devices: 92 us -> none  [the longest x1 92 us: local(): lax.all_to_all(stacked, FSDP, split_axis=1, concat_axis=1, tiled=True)]
    reduce_scatter x1 -> x0, waiting for transfers between devices: 54.8 us -> none  [local(): lax.psum_scatter(partials[0].astype(jnp.float32).astype(jnp.bfloat16), RE...]
    all_to_all x2 -> x0, starting transfers between devices: 17.6 us -> none  [the longest x1 10.3 us: local(): lax.all_to_all(outgoing, FSDP, split_axis=1, concat_axis=1, tiled=True)]
    unnamed x49 -> x13, local copies, waits for them, and re-layouts: 10.9 us -> 2.54 us
    dot_general x2 -> x1, matrix products: 8.72 us -> 3.22 us  [precondition(): jnp.dot(gradient, projected, preferred_element_type=jnp.float32)]
    dot_general x20 -> x10, matrix products: 9.84 us -> 4.34 us  [inverse_root(): jnp.dot(inverse, current, precision=lax.Precision.HIGHEST)]
  transfers between devices with their start and end apart: 3 -> 0, of which waited for: 2 -> 0; matrix products, arithmetic and copies ran while one was open for 2% -> 0% of each run, Pallas kernels for 0% -> 0%
where the time goes in v1:
time: 177 us; the launch traced here: 176 us
  Pallas kernels  132 us (75%)
  matrix products  28.1 us (16%)
  other arithmetic  8.7 us (5%)
  local copies, waits for them, and re-layouts  3.84 us (2%)
  between operations  3.09 us (2%)
    pallas_call x1, Pallas kernels, local(): pl.pallas_call(functools.partial(gather_kernel, nf, nr), out_shape=(jax.S...  71.2 us
    pallas_call x1, Pallas kernels, local(): pl.pallas_call(functools.partial(scatter_kernel, nf, nr), out_shape=(jax....  61.2 us
    dot_general x10, matrix products, inverse_root(): jnp.dot(inverse, current, precision=lax.Precision.HIGHEST)  4.34 us
    dot_general x8, matrix products, inverse_root(): current = jnp.dot(current, middle, precision=lax.Precision.HIGHEST)  3.69 us
    dot_general x10, matrix products, inverse_root(): inverse = jnp.dot(middle, inverse, precision=lax.Precision.HIGHEST)  3.58 us

profile of v1, /device:TPU:2, one launch (start us, length us, event | category | flops | bytes accessed | tf_op | source)
XLA Modules:
  0.0 176.2 jit_solution(9393821189788870313)
XLA Ops:
  0.6 1.4 fusion.27
  2.0 0.1 convert_reduce_fusion
  2.1 0.5 multiply_add_fusion.slot_ref
  2.6 0.7 fusion.28
  3.3 0.7 select_reduce_fusion.2.back_ref
  4.0 0.6 iota_compare_fusion.8
  4.7 71.2 %shard_map.50 = (bf16[32,32,1024]{2,1,0:T(8,128)(2,1)}, bf16[32,32,256]{2,1,0:T(8,128)(2,1)}, f32[8,128]{1,0:T(8,128)}) custom-call(s32[14]{0:T(128)} %multiply_add_fusion.slot_ref, bf16[8,2,7,32,1024]{4,3,2,1,0:T(8,128)(2,1)} %bitcast.103, bf16[2,1024,256]{2,1,0:T(8,128)(2,1)} %bitcast.104), custom_call_target="tpu_custom_call" | custom-call | tf_op jit(solution)/shard_map/pallas_call | solution.py:319
  75.9 1.3 reduce_sum.57
  77.8 0.0 copy-start.5
  77.9 2.2 %multiply_convert_fusion = bf16[32,32,1024]{2,1,0:T(8,128)(2,1)S(1)} fusion(bf16[32,32,1024]{2,1,0:T(8,128)(2,1)} %get-tuple-element.8, f32[]{:T(128)S(6)} %min_shard_map.3), kind=kLoop, calls=%fused_computation.1 | loop fusion | flops 3145728 | bytes 4194308 | tf_op jit(solution)/shard_map/convert_element_type | solution.py:353
  80.1 0.0 copy-start
  80.1 1.3 copy-done
  81.4 0.0 copy-done.5
  81.4 3.2 %fusion.14 = f32[1024,256]{1,0:T(8,128)} fusion(bf16[1024,1024]{1,0:T(8,128)(2,1)S(1)} %bitcast.99, bf16[32,32,1024]{2,1,0:T(8,128)(2,1)S(1)} %multiply_convert_fusion, bf16[32,32,256]{2,1,0:T(8,128)(2,1)S(1)} %copy-done.5), kind=kOutput, calls=%fused_computation.36 | convolution fusion | flops 1074003968 | bytes 5767168 | tf_op jit(solution)/shard_map/dot_general | solution.py:43
  84.7 2.0 %fusion = f32[1024,256]{1,0:T(8,128)S(1)} fusion(f32[1024,256]{1,0:T(8,128)} %fusion.14, bf16[1024,256]{1,0:T(8,128)(2,1)S(1)} %bitcast.108, bf16[32,32,256]{2,1,0:T(8,128)(2,1)S(1)} %copy-done.5), kind=kOutput, calls=%fused_computation.4 | convolution fusion | flops 269025280 | bytes 3145728 | tf_op jit(solution)/shard_map/dot_general | solution.py:41
  86.7 2.4 %select_reduce_fusion.1 = (f32[]{:T(128)}, f32[256,256]{1,0:T(8,128)S(1)}) fusion(f32[1024,256]{1,0:T(8,128)S(1)} %fusion), kind=kOutput, calls=%fused_computation.42 | convolution fusion | flops 805502976 | bytes 1310724 | tf_op jit(solution)/shard_map/dot_general | solution.py:44
  89.8 0.3 fusion.12
  90.2 0.4 fusion.22
  90.6 0.3 fusion.19
  90.8 0.4 fusion.11
  91.2 0.4 fusion.41
  91.6 0.4 fusion.40
  92.0 0.4 fusion.10
  92.4 0.4 fusion.43
  92.8 0.4 fusion.42
  93.2 0.4 fusion.9
  93.6 0.4 fusion.44
  93.9 0.4 fusion.45
  94.3 0.4 fusion.8
  94.7 0.4 convolution_divide_fusion.1
  95.1 0.0 copy-start.1
  95.1 1.0 fusion.46
  96.1 0.3 fusion.34
  96.5 0.2 copy-done.1
  96.7 0.8 convolution_convert_fusion.2
  97.5 0.6 fusion.47
  98.0 1.2 select_reduce_fusion
  99.9 1.0 fusion.6
  100.9 1.0 fusion.23
  102.0 0.3 fusion.18
  102.2 0.4 fusion.5
  102.6 0.4 fusion.49
  103.0 0.4 fusion.48
  103.4 0.4 fusion.4
  103.8 0.4 fusion.51
  104.2 0.4 fusion.50
  104.6 0.4 fusion.3
  105.0 0.4 fusion.52
  105.3 0.4 fusion.53
  105.7 0.0 copy-start.2
  105.7 0.4 fusion.2
  106.1 0.4 convolution_divide_fusion
  106.5 0.4 fusion.54
  106.9 0.6 convolution_convert_fusion.1
  107.5 0.0 copy-done.2
  107.6 2.1 %add_convert_fusion = bf16[1024,1024]{1,0:T(8,128)(2,1)} fusion(bf16[1024,1024]{1,0:T(8,128)(2,1)S(1)} %bitcast.101, bf16[1024,256]{1,0:T(8,128)(2,1)S(1)} %convolution_convert_fusion.1, f32[1024,256]{1,0:T(8,128)S(1)} %fusion.46), kind=kOutput, calls=%fused_computation | convolution fusion | flops 540278784 | bytes 5767168 | tf_op jit(solution)/shard_map/dot_general | solution.py:67
  109.7 1.8 %convolution_convert_fusion = bf16[1024,256]{1,0:T(8,128)(2,1)} fusion(f32[1024,256]{1,0:T(8,128)S(1)} %fusion.46, f32[256,256]{1,0:T(8,128)S(1)} %fusion.54), kind=kOutput, calls=%fused_computation.6 | convolution fusion | flops 805568512 | bytes 1835008 | tf_op jit(solution)/shard_map/dot_general | solution.py:58
  111.5 61.2 %shard_map.51 = (bf16[14,32,1024]{2,1,0:T(8,128)(2,1)}, bf16[32,2,32,256]{3,2,1,0:T(8,128)(2,1)}) custom-call(s32[64]{0:T(128)} %select_reduce_fusion.2.back_ref, bf16[32,32,1024]{2,1,0:T(8,128)(2,1)} %bitcast.102, bf16[32,32,256]{2,1,0:T(8,128)(2,1)} %bitcast.106), custom_call_target="tpu_custom_call" | custom-call | tf_op jit(solution)/shard_map/pallas_call | solution.py:356
  172.7 1.3 copy.6
  174.0 0.0 copy-start.4
  174.0 0.0 copy-done.3
  174.0 1.2 broadcast_select_fusion
  175.2 0.0 copy-done.4
  175.2 0.9 copy.8
  (1 shorter events, 0.0 us)
Async XLA Ops:
  77.8 3.6 %copy-start.5 = (bf16[32,32,256]{2,1,0:T(8,128)(2,1)S(1)}, bf16[32,32,256]{2,1,0:T(8,128)(2,1)}, u32[]{:S(2)}) copy-start(bf16[32,32,256]{2,1,0:T(8,128)(2,1)} %get-tuple-element.9) | copy-start | bytes 1572868
  80.1 1.4 copy-start
  95.1 1.6 copy-start.1
  105.7 1.8 %copy-start.2 = (bf16[32,32,1024]{2,1,0:T(8,128)(2,1)S(1)}, bf16[32,32,1024]{2,1,0:T(8,128)(2,1)}, u32[]{:S(2)}) copy-start(bf16[32,32,1024]{2,1,0:T(8,128)(2,1)} %copy-done) | copy-start | bytes 6291460
  111.5 62.6 %copy-start.3 = (bf16[1,1,2,1024,256]{4,3,2,1,0:T(8,128)(2,1)S(1)}, bf16[1,1,2,1024,256]{4,3,2,1,0:T(8,128)(2,1)}, u32[]{:S(2)}) copy-start(bf16[1,1,2,1024,256]{4,3,2,1,0:T(8,128)(2,1)} %param.4) | copy-start | bytes 3145732
  174.0 1.2 copy-start.4

commit v2 on v1

v2 whole, which is shorter than its diff:
```python
import functools
import math

import jax
import jax.numpy as jnp
from jax import lax
from jax.experimental import pallas as pl
from jax.experimental.pallas import tpu as pltpu
from jax.sharding import PartitionSpec as P

NS_ITERS = 5
DECAY = 0.9
DAMPING = 64.0
LAST_AXES = (((1,), (1,)), ((), ()))
MESH = pl.DeviceIdType.MESH
F32 = jnp.float32
BF16 = jnp.bfloat16


def dot(a, b, dims=(((1,), (0,)), ((), ()))):
    return lax.dot_general(a, b, dims, preferred_element_type=F32)


def split(value):
    high = value.astype(BF16)
    return high, (value - high.astype(F32)).astype(BF16)


def inverse_root(matrix, epsilon, eye):
    trace = jnp.sum(jnp.sum(matrix * eye, axis=1, keepdims=True), axis=0, keepdims=True) + epsilon
    state = matrix * (1.0 / trace)
    inverse = 1.5 * eye - 0.5 * state
    for step in range(1, NS_ITERS):
        low = state.astype(BF16)
        half = 1.5 * state - 0.5 * dot(low, low)
        state = 1.5 * half - 0.5 * dot(low, half.astype(BF16))
        low = state.astype(BF16)
        high_part, low_part = split(inverse)
        inverse = 1.5 * inverse - 0.5 * (dot(low, high_part) + dot(low, low_part))
    return inverse * (1.0 / jnp.sqrt(trace))


def wait_bytes(ref, sem):
    pltpu.make_async_copy(ref, ref, sem).wait()


def put(src, dst, send, recv, device):
    pltpu.make_async_remote_copy(
        src_ref=src, dst_ref=dst, send_sem=send, recv_sem=recv, device_id=device, device_id_type=MESH
    ).start()


def barrier_with(f, r, nf, nr, with_rep):
    barrier = pltpu.get_barrier_semaphore()

    def to_fsdp(i, carry):
        pl.semaphore_signal(barrier, inc=1, device_id=(lax.rem(f + i, nf), r), device_id_type=MESH)
        return carry

    def to_rep(i, carry):
        pl.semaphore_signal(barrier, inc=1, device_id=(f, lax.rem(r + i, nr)), device_id_type=MESH)
        return carry

    lax.fori_loop(1, nf, to_fsdp, 0)
    if with_rep:
        lax.fori_loop(1, nr, to_rep, 0)
    pl.semaphore_wait(barrier, nf - 1 + (nr - 1 if with_rep else 0))


def step_kernel(
    nf, nr, limit, table, part, sk, upd_out, nk_out,
    own, rc, s_a, r_a, s_b, r_b, fin, sk_r, sk_s, ss_a, ss_b, g_out, z_out, base, first,
    gs, zt, at, wh, wl, wth, wtl, qb, qt, ht, up, new, s_r, s_x, slots, back,
    own_sem, rc_sem, ra_sem, rb_sem, gz_sem, send_sem, out_sem,
):
    f = lax.axis_index("fsdp")
    r = lax.axis_index("rep")
    ny = nr // 2
    steps = own.shape[2]
    rows = own.shape[3]
    y = r // 2
    c = lax.rem(r, 2)
    partner = (f, 2 * y + 1 - c)
    ydev = ((f, 2 * lax.rem(y + 1, ny) + c), (f, 2 * lax.rem(y + ny - 1, ny) + c))
    rel = (1, ny - 1)

    def place(j):
        n = 2 * j + c
        return n + (n + 4) // 8

    spot = f - (f + 5) // 9
    busy = (lax.rem(f + 5, 9) != 0) & (lax.rem(spot, 2) == c)
    block = spot // 2

    for d in (2, 1, 3, 0):
        pltpu.make_async_copy(part.at[2 * lax.rem(y + d, ny) + c], own.at[d], own_sem.at[d]).start()

    barrier_with(f, r, nf, nr, True)

    def order(i):
        return lax.rem(f + i, steps)

    for i in range(steps):
        k = order(i)
        for d in (2, 1, 3, 0):
            put(part.at[2 * lax.rem(y + d, ny) + 1 - c, :, k], rc.at[d, :, k], send_sem.at[0], rc_sem.at[d, k], partner)
        if i == 0:
            def spread(i, carry):
                t = lax.rem(f + i, nf)
                put(sk.at[:, pl.ds(pl.multiple_of(t * rows, rows), rows), :], sk_r.at[f], send_sem.at[1], gz_sem.at[0], (t, r))
                return carry

            lax.fori_loop(1, nf, spread, 0)
            mine = pltpu.make_async_copy(sk.at[:, pl.ds(pl.multiple_of(f * rows, rows), rows), :], sk_r.at[f], gz_sem.at[3])
            mine.start()

    count = 2 * steps
    owners = [table[r * count + j] for j in range(count)]
    for j in range(count):
        slots[j] = 2 * owners[j] + sum(((owners[i] == owners[j]).astype(jnp.int32) for i in range(j)), jnp.int32(0))

    def invert(t, carry):
        at = jnp.int32(0)
        for j in range(count):
            at = jnp.where(slots[j] == t, j, at)
        back[t] = at
        return carry

    lax.fori_loop(0, 2 * nf, invert, 0)

    for d in (2, 1, 3, 0):
        pltpu.make_async_copy(own.at[d], own.at[d], own_sem.at[d]).wait()

    def both(d, h, k):
        return own[d, h, k].astype(F32) + rc[d, h, k].astype(F32)

    def opposite(k):
        wait_bytes(rc.at[2, :, k], rc_sem.at[2, k])
        for d in (0, 1):
            s_a[d, k] = both(2, d, k).astype(BF16)
            put(s_a.at[d, k], r_a.at[d, k], send_sem.at[2], ra_sem.at[d, k], ydev[d])

    def independent(k):
        for d in (0, 1):
            wait_bytes(rc.at[rel[d], :, k], rc_sem.at[rel[d], k])
            s_b[d, 1 - d, k] = both(rel[d], 1 - d, k).astype(BF16)
            put(s_b.at[d, 1 - d, k], r_b.at[d, 1 - d, k], send_sem.at[3], rb_sem.at[d, 1 - d, k], ydev[d])

    def dependent(k):
        for d in (0, 1):
            wait_bytes(r_a.at[d, k], ra_sem.at[d, k])
            s_b[d, d, k] = (both(rel[d], d, k) + r_a[d, k].astype(F32)).astype(BF16)
            put(s_b.at[d, d, k], r_b.at[d, d, k], send_sem.at[3], rb_sem.at[d, d, k], ydev[d])

    def final(k, total):
        wait_bytes(rc.at[0, :, k], rc_sem.at[0, k])
        for h in (0, 1):
            wait_bytes(r_b.at[1 - h, h, k], rb_sem.at[1 - h, h, k])
            wait_bytes(r_b.at[h, h, k], rb_sem.at[h, h, k])
            value = (both(0, h, k) + (r_b[0, h, k].astype(F32) + r_b[1, h, k].astype(F32))).astype(BF16)
            fin[h, k] = value
            target = place(h * steps + k)

            @pl.when(target != f)
            def _():
                put(fin.at[h, k], g_out.at[f], send_sem.at[4], gz_sem.at[1], (target, r))

            @pl.when(target == f)
            def _():
                g_out[f] = value

            wide = value.astype(F32)
            square = wide * wide
            total = total + jnp.sum(square.reshape(rows // 8, 8, square.shape[1] // 128, 128).transpose(0, 2, 1, 3).reshape(-1, 8, 128), axis=0)
        return total

    def sketches():
        mine.wait()
        wait_bytes(sk_r.at[pl.ds(0, nf - 1)], gz_sem.at[0])
        for i in range(2 * steps):
            j = lax.rem(f + i, 2 * steps)
            target = place(j)
            slot = slots[j]
            sk_s[j] = sk_r[slot // 2, lax.rem(slot, 2)]

            @pl.when(target != f)
            def _():
                put(sk_s.at[j], z_out.at[f], send_sem.at[6], gz_sem.at[2], (target, r))

            @pl.when(target == f)
            def _():
                z_out[f] = sk_s[j]

    total = jnp.zeros((8, 128), F32)
    for i in range(steps + 3):
        if i < steps:
            opposite(order(i))
        if 1 <= i < steps + 1:
            independent(order(i - 1))
        if 2 <= i < steps + 2:
            dependent(order(i - 2))
        if i == steps + 1:
            sketches()
        if i >= 3:
            total = final(order(i - 3), total)

    ss_a[r] = total

    def rep_send(i, carry):
        put(ss_a.at[r], ss_a.at[r], send_sem.at[5], gz_sem.at[4], (f, lax.rem(r + i, nr)))
        return carry

    lax.fori_loop(1, nr, rep_send, 0)
    wait_bytes(ss_a.at[pl.ds(0, nr - 1)], gz_sem.at[4])
    ss_b[f] = jnp.sum(ss_a[...], axis=0)

    def fsdp_send(i, carry):
        put(ss_b.at[f], ss_b.at[f], send_sem.at[7], gz_sem.at[5], (lax.rem(f + i, nf), r))
        return carry

    lax.fori_loop(1, nf, fsdp_send, 0)

    width, rank = g_out.shape[2], z_out.shape[2]

    @pl.when(busy)
    def _():
        wait_bytes(z_out.at[pl.ds(0, nf - 1)], gz_sem.at[2])
        held = z_out[...].reshape(width, rank)
        zt[...] = held.T
        gram = dot(zt[...], held).astype(BF16)
        base[...] = DECAY * dot(held, gram)
        wait_bytes(g_out.at[pl.ds(0, nf - 1)], gz_sem.at[1])
        first[...] = dot(zt[...], g_out[...].reshape(width, width))

    wait_bytes(ss_b.at[pl.ds(0, nf - 1)], gz_sem.at[5])

    @pl.when(busy)
    def _():
        eye = (
            lax.broadcasted_iota(jnp.int32, (rank, rank), 0) == lax.broadcasted_iota(jnp.int32, (rank, rank), 1)
        ).astype(F32)
        held = z_out[...].reshape(width, rank)
        squares = jnp.sum(ss_b[...], axis=0)
        squares = jnp.sum(jnp.sum(squares, axis=1, keepdims=True), axis=0, keepdims=True)
        clip = jnp.minimum(1.0, limit / jnp.sqrt(squares + 1e-06))
        gs[...] = (clip * g_out[...].reshape(width, width).astype(F32)).astype(BF16)
        at[...] = (clip * first[...]).astype(BF16)
        powered = base[...] + dot(gs[...], at[...], LAST_AXES)
        high, low = split(powered)
        wh[...] = high
        wl[...] = low
        wth[...] = high.T
        wtl[...] = low.T
        inner = dot(wth[...], wh[...]) + (dot(wth[...], wl[...]) + dot(wtl[...], wh[...]))
        root_h, root_l = split(inverse_root(inner, 1e-06, eye))
        qb[...] = (dot(wh[...], root_h) + (dot(wh[...], root_l) + dot(wl[...], root_h))).astype(BF16)
        qt[...] = (dot(root_h, wth[...]) + (dot(root_l, wth[...]) + dot(root_h, wtl[...]))).astype(BF16)
        ht[...] = dot(qt[...], gs[...]).astype(BF16)
        align_h, align_l = split(dot(qt[...], held))
        cross = dot(align_h, align_l, LAST_AXES)
        energy = DECAY * (dot(align_h, align_h, LAST_AXES) + (cross + cross.T)) + dot(ht[...], ht[...], LAST_AXES)
        inverse = inverse_root(energy + DAMPING * eye, 0.0, eye)
        energy_h, energy_l = split(energy)
        inverse_h, inverse_l = split(inverse)
        inner_part = dot(energy_h, inverse_h) + (dot(energy_h, inverse_l) + dot(energy_l, inverse_h))
        new[...] = dot(qb[...], inner_part.astype(BF16)).astype(BF16).reshape(nf, rows, rank)

        def send_new(i, carry):
            t = lax.rem(f + i, nf)
            put(new.at[t], s_r.at[block], out_sem.at[0], out_sem.at[1], (t, r))
            return carry

        def send_up(i, carry):
            t = lax.rem(f + i, nf)
            put(up.at[t], upd_out.at[block], out_sem.at[2], out_sem.at[3], (t, r))
            return carry

        lax.fori_loop(1, nf, send_new, 0)
        mix_h, mix_l = split(math.sqrt(DAMPING) * inverse - eye)
        ft = (dot(mix_h, ht[...]) + dot(mix_l, ht[...])).astype(BF16)
        up[...] = (gs[...].astype(F32) + dot(qb[...], ft)).astype(BF16).reshape(nf, rows, width)
        lax.fori_loop(1, nf, send_up, 0)
        s_r[block] = new[f]
        upd_out[block] = up[f]
        wait_bytes(s_r.at[pl.ds(0, count - 1)], out_sem.at[1])

    @pl.when(jnp.logical_not(busy))
    def _():
        wait_bytes(s_r, out_sem.at[1])

    def scatter(i, carry):
        t = lax.rem(f + i, nf)
        for q in (0, 1):
            s_x[t, q] = s_r[back[2 * t + q]]
        put(s_x.at[t], nk_out.at[:, f], out_sem.at[4], out_sem.at[5], (t, r))
        return carry

    lax.fori_loop(1, nf, scatter, 0)
    for q in (0, 1):
        nk_out[q, f] = s_r[back[2 * f + q]]

    wait_bytes(rc, send_sem.at[0])
    wait_bytes(sk_r.at[pl.ds(0, nf - 1)], send_sem.at[1])
    wait_bytes(s_a, send_sem.at[2])
    wait_bytes(s_b, send_sem.at[3])
    wait_bytes(ss_a.at[pl.ds(0, nr - 1)], send_sem.at[5])
    wait_bytes(ss_b.at[pl.ds(0, nf - 1)], send_sem.at[7])
    wait_bytes(s_x.at[pl.ds(0, nf - 1)], out_sem.at[4])
    wait_bytes(nk_out.at[:, pl.ds(0, nf - 1)], out_sem.at[5])

    @pl.when(busy)
    def _():
        wait_bytes(g_out.at[pl.ds(0, count - 1)], send_sem.at[4])
        wait_bytes(z_out.at[pl.ds(0, count - 1)], send_sem.at[6])
        wait_bytes(new.at[pl.ds(0, nf - 1)], out_sem.at[0])
        wait_bytes(up.at[pl.ds(0, nf - 1)], out_sem.at[2])
        wait_bytes(upd_out.at[pl.ds(0, count - 1)], out_sem.at[3])

    @pl.when(jnp.logical_not(busy))
    def _():
        wait_bytes(g_out.at[pl.ds(0, count)], send_sem.at[4])
        wait_bytes(z_out.at[pl.ds(0, count)], send_sem.at[6])
        wait_bytes(upd_out, out_sem.at[3])


def local(nf, nr, partials, sketch, owner_table):
    blocks_all, rows, width = partials.shape[1:]
    per_slice = blocks_all // nr
    half = per_slice // 2
    rank = sketch.shape[4]
    ny = nr // 2
    vmem = pl.BlockSpec(memory_space=pltpu.VMEM)
    anyw = pl.BlockSpec(memory_space=pl.ANY)
    smem = pl.BlockSpec(memory_space=pltpu.SMEM)
    dma = pltpu.SemaphoreType.DMA
    tall, wide = pltpu.VMEM((width, rank), BF16), pltpu.VMEM((rank, width), BF16)
    held = sketch[0, 0]
    upd, fresh = pl.pallas_call(
        functools.partial(step_kernel, nf, nr, 0.5 * math.sqrt(blocks_all * width * width)),
        out_shape=(
            jax.ShapeDtypeStruct((per_slice, rows, width), BF16),
            jax.ShapeDtypeStruct((2, nf, rows, rank), BF16),
        ),
        in_specs=[smem, anyw, anyw],
        out_specs=(vmem, vmem),
        scratch_shapes=[
            pltpu.VMEM((ny, 2, half, rows, width), BF16),
            pltpu.VMEM((ny, 2, half, rows, width), BF16),
            pltpu.VMEM((2, half, rows, width), BF16),
            pltpu.VMEM((2, half, rows, width), BF16),
            pltpu.VMEM((2, 2, half, rows, width), BF16),
            pltpu.VMEM((2, 2, half, rows, width), BF16),
            pltpu.VMEM((2, half, rows, width), BF16),
            pltpu.VMEM((nf, 2, rows, rank), BF16),
            pltpu.VMEM((per_slice, rows, rank), BF16),
            pltpu.VMEM((nr, 8, 128), F32),
            pltpu.VMEM((nf, 8, 128), F32),
            pltpu.VMEM((nf, rows, width), BF16),
            pltpu.VMEM((nf, rows, rank), BF16),
            pltpu.VMEM((width, rank), F32),
            pltpu.VMEM((rank, width), F32),
            pltpu.VMEM((width, width), BF16),
            wide, wide, tall, tall, wide, wide, tall, wide, wide,
            pltpu.VMEM((nf, rows, width), BF16),
            pltpu.VMEM((nf, rows, rank), BF16),
            pltpu.VMEM((per_slice, rows, rank), BF16),
            pltpu.VMEM((nf, 2, rows, rank), BF16),
            pltpu.SMEM((per_slice,), jnp.int32),
            pltpu.SMEM((2 * nf,), jnp.int32),
            dma((ny,)),
            dma((ny, half)),
            dma((2, half)),
            dma((2, 2, half)),
            dma((6,)),
            dma((8,)),
            dma((6,)),
        ],
        compiler_params=pltpu.CompilerParams(collective_id=0, has_side_effects=True),
    )(owner_table[:, 0], partials.reshape(nr, 2, half, rows, width), held)

    owners = lax.dynamic_slice_in_dim(owner_table[:, 0], lax.axis_index("rep") * per_slice, per_slice)
    filled = jnp.sum((owners == lax.axis_index("fsdp")).astype(jnp.int32))
    keep = jnp.arange(2, dtype=jnp.int32)[:, None, None] < filled
    return upd, jnp.where(keep, fresh.reshape(2, width, rank), held)[None, None]


def solution(mesh):
    nf, nr = mesh.shape["fsdp"], mesh.shape["rep"]
    return jax.shard_map(
        functools.partial(local, nf, nr),
        mesh=mesh,
        in_specs=(P("rep", None, "fsdp", None), P("fsdp", "rep", None, None, None), P()),
        out_specs=(P("rep", "fsdp", None), P("fsdp", "rep", None, None, None)),
        check_vma=False,
    )
```

time: 177 us -> 140 us (0.79)
  matrix products: 28.1 us -> 0 us
  other arithmetic: 8.7 us -> 4.47 us
  between operations: 3.09 us -> 0.67 us
    dot_general x40 -> x0, matrix products: 28.1 us -> none  [the longest x10 4.34 us: inverse_root(): jnp.dot(inverse, current, precision=lax.Precision.HIGHEST)]
    convert_element_type x1 -> x0, other arithmetic: 2.22 us -> none  [local(): (clip_factor * g_rows.reshape(width, width).astype(F32)).astype(BF16)]
    reduce_sum x3 -> x0, other arithmetic: 2.03 us -> none  [the longest x1 1.28 us: local(): sum_squares = jnp.sum(squares)]
    pallas_call x2 -> x1, Pallas kernels: 132 us -> 132 us  [local(): pl.pallas_call(functools.partial(step_kernel, nf, nr, 0.5 * math.sqrt(blo...]
where the time goes in v2:
time: 140 us; the launch traced here: 139 us
  Pallas kernels  132 us (94%)
  other arithmetic  4.47 us (3%)
  local copies, waits for them, and re-layouts  2.17 us (2%)
    pallas_call x1, Pallas kernels, local(): pl.pallas_call(functools.partial(step_kernel, nf, nr, 0.5 * math.sqrt(blo...  132 us

profile of v2, /device:TPU:2, one launch (start us, length us, event | category | flops | bytes accessed | tf_op | source)
XLA Modules:
  0.0 139.1 jit_solution(13668481818331388351)
XLA Ops:
  0.6 0.0 copy-start
  0.6 1.5 %fusion = s32[]{:T(128)} fusion(s32[112,1]{0,1:T(1,128)} %param.5, s32[]{:T(128)S(6)} %select_n.8, s32[]{:T(128)S(6)} %axis_index.25), kind=kLoop, calls=%fused_computation.2 | loop fusion | flops 41 | bytes 68 | tf_op jit(solution)/shard_map/reduce_sum | solution.py:382
  2.1 0.6 iota_compare_fusion
  2.8 131.8 %shard_map.50 = (bf16[14,32,1024]{2,1,0:T(8,128)(2,1)}, bf16[2,32,32,256]{3,2,1,0:T(8,128)(2,1)}) custom-call(s32[112]{0:T(128)} %bitcast.7, bf16[8,2,7,32,1024]{4,3,2,1,0:T(8,128)(2,1)} %bitcast.4, bf16[2,1024,256]{2,1,0:T(8,128)(2,1)} %bitcast.5), custom_call_target="tpu_custom_call" | custom-call | tf_op jit(solution)/shard_map/pallas_call | solution.py:338
  134.6 0.0 copy-done
  134.6 2.4 %broadcast_select_fusion = bf16[1,1,2,1024,256]{4,3,2,1,0:T(8,128)(2,1)} fusion(bf16[1,1,2,1024,256]{4,3,2,1,0:T(8,128)(2,1)} %bitcast.6, bf16[1,1,2,1024,256]{4,3,2,1,0:T(8,128)(2,1)S(1)} %copy-done, pred[2]{0:T(512)(128)(4,1)S(1)} %iota_compare_fusion), kind=kLoop, calls=%fused_computation | loop fusion | flops 524288 | bytes 3145730 | tf_op jit(solution)/shard_map/jit(_where)/select_n | solution.py:384
  136.9 2.2 %copy.6 = bf16[14,32,1024]{2,1,0:T(8,128)(2,1)} copy(bf16[14,32,1024]{2,1,0:T(8,128)(2,1)} %get-tuple-element.8) | data formatting | bytes 1835008
Async XLA Ops:
  0.6 133.9 %copy-start = (bf16[1,1,2,1024,256]{4,3,2,1,0:T(8,128)(2,1)S(1)}, bf16[1,1,2,1024,256]{4,3,2,1,0:T(8,128)(2,1)}, u32[]{:S(2)}) copy-start(bf16[1,1,2,1024,256]{4,3,2,1,0:T(8,128)(2,1)} %param.4) | copy-start | bytes 3145732

commit v3 on v2

--- a/solution.py
+++ b/solution.py
@@ -69,7 +69,7 @@
 
 def step_kernel(
     nf, nr, limit, table, part, sk, upd_out, nk_out,
-    own, rc, s_a, r_a, s_b, r_b, fin, sk_r, sk_s, ss_a, ss_b, g_out, z_out, base, first,
+    own, rc, s_a, r_a, s_b, r_b, fin, sk_r, sk_s, ss_a, ss_b, g_out, z_out, z_in, base, first,
     gs, zt, at, wh, wl, wth, wtl, qb, qt, ht, up, new, s_r, s_x, slots, back,
     own_sem, rc_sem, ra_sem, rb_sem, gz_sem, send_sem, out_sem,
 ):
@@ -80,6 +80,10 @@
     rows = own.shape[3]
     y = r // 2
     c = lax.rem(r, 2)
+    z_one = z_out.reshape(z_out.shape[0] * z_out.shape[1], *z_out.shape[2:])
+    nx, nz, npiece = 4, nf // 4, nf // 2
+    prow = sk_r.shape[2]
+    z, x = f // nx, lax.rem(f, nx)
     partner = (f, 2 * y + 1 - c)
     ydev = ((f, 2 * lax.rem(y + 1, ny) + c), (f, 2 * lax.rem(y + ny - 1, ny) + c))
     rel = (1, ny - 1)
@@ -104,15 +108,25 @@
         k = order(i)
         for d in (2, 1, 3, 0):
             put(part.at[2 * lax.rem(y + d, ny) + 1 - c, :, k], rc.at[d, :, k], send_sem.at[0], rc_sem.at[d, k], partner)
-        if i == 0:
-            def spread(i, carry):
-                t = lax.rem(f + i, nf)
-                put(sk.at[:, pl.ds(pl.multiple_of(t * rows, rows), rows), :], sk_r.at[f], send_sem.at[1], gz_sem.at[0], (t, r))
-                return carry
-
-            lax.fori_loop(1, nf, spread, 0)
-            mine = pltpu.make_async_copy(sk.at[:, pl.ds(pl.multiple_of(f * rows, rows), rows), :], sk_r.at[f], gz_sem.at[3])
-            mine.start()
+
+    def away(level):
+        return jnp.where(lax.rem(level, 2) == 0, 2, nz - 2)
+
+    def near(i, two):
+        level = lax.rem(z + jnp.where(i // nx == 3, two, (0, 1, nz - 1, 0)[i // nx]), nz)
+        return level, level * nx + lax.rem(x + i % nx, nx)
+
+    def piece_of(t):
+        return lax.rem(t, npiece)
+
+    def cut(t):
+        return pl.ds(pl.multiple_of(piece_of(t) * prow, prow), prow)
+
+    mine = pltpu.make_async_copy(sk.at[:, cut(f), :], sk_r.at[f], gz_sem.at[3])
+    mine.start()
+    for i in range(npiece - 1, 0, -1):
+        level, t = near(i, nz - away(z))
+        put(sk.at[:, cut(t), :], sk_r.at[f], send_sem.at[1], gz_sem.at[0], (t, r))
 
     count = 2 * steps
     owners = [table[r * count + j] for j in range(count)]
@@ -176,20 +190,23 @@
 
     def sketches():
         mine.wait()
-        wait_bytes(sk_r.at[pl.ds(0, nf - 1)], gz_sem.at[0])
+        wait_bytes(sk_r.at[pl.ds(0, npiece - 1)], gz_sem.at[0])
         for i in range(2 * steps):
             j = lax.rem(f + i, 2 * steps)
             target = place(j)
             slot = slots[j]
-            sk_s[j] = sk_r[slot // 2, lax.rem(slot, 2)]
+            owner = slot // 2
+            apart = lax.rem(owner // nx - z + nz, nz)
+            here = (apart <= 1) | (apart == nz - 1) | (apart == away(z))
+            sk_s[j] = sk_r[jnp.where(here, owner, f), lax.rem(slot, 2)]
 
             @pl.when(target != f)
             def _():
-                put(sk_s.at[j], z_out.at[f], send_sem.at[6], gz_sem.at[2], (target, r))
+                put(sk_s.at[j], z_out.at[f // npiece, piece_of(f)], send_sem.at[6], gz_sem.at[2], (target, r))
 
             @pl.when(target == f)
             def _():
-                z_out[f] = sk_s[j]
+                z_out[f // npiece, piece_of(f)] = sk_s[j]
 
     total = jnp.zeros((8, 128), F32)
     for i in range(steps + 3):
@@ -220,12 +237,17 @@
 
     lax.fori_loop(1, nf, fsdp_send, 0)
 
-    width, rank = g_out.shape[2], z_out.shape[2]
+    width, rank = g_out.shape[2], sk_r.shape[3]
 
     @pl.when(busy)
     def _():
-        wait_bytes(z_out.at[pl.ds(0, nf - 1)], gz_sem.at[2])
-        held = z_out[...].reshape(width, rank)
+        wait_bytes(z_one.at[pl.ds(0, nf - 1)], gz_sem.at[2])
+        level = slots[block] // (2 * nx)
+        for k in range(nz // 2):
+            apart = lax.rem(k - level + nz, nz)
+            low = (apart <= 1) | (apart == nz - 1) | (apart == nz - away(level))
+            z_in[k * nx : (k + 1) * nx] = z_out[jnp.where(low, 0, 1), k * nx : (k + 1) * nx]
+        held = z_in[...].reshape(width, rank)
         zt[...] = held.T
         gram = dot(zt[...], held).astype(BF16)
         base[...] = DECAY * dot(held, gram)
@@ -239,7 +261,7 @@
         eye = (
             lax.broadcasted_iota(jnp.int32, (rank, rank), 0) == lax.broadcasted_iota(jnp.int32, (rank, rank), 1)
         ).astype(F32)
-        held = z_out[...].reshape(width, rank)
+        held = z_in[...].reshape(width, rank)
         squares = jnp.sum(ss_b[...], axis=0)
         squares = jnp.sum(jnp.sum(squares, axis=1, keepdims=True), axis=0, keepdims=True)
         clip = jnp.minimum(1.0, limit / jnp.sqrt(squares + 1e-06))
@@ -263,11 +285,11 @@
         energy_h, energy_l = split(energy)
         inverse_h, inverse_l = split(inverse)
         inner_part = dot(energy_h, inverse_h) + (dot(energy_h, inverse_l) + dot(energy_l, inverse_h))
-        new[...] = dot(qb[...], inner_part.astype(BF16)).astype(BF16).reshape(nf, rows, rank)
+        new[...] = dot(qb[...], inner_part.astype(BF16)).astype(BF16).reshape(npiece, prow, rank)
 
         def send_new(i, carry):
             t = lax.rem(f + i, nf)
-            put(new.at[t], s_r.at[block], out_sem.at[0], out_sem.at[1], (t, r))
+            put(new.at[piece_of(t)], s_r.at[block], out_sem.at[0], out_sem.at[1], (t, r))
             return carry
 
         def send_up(i, carry):
@@ -280,7 +302,7 @@
         ft = (dot(mix_h, ht[...]) + dot(mix_l, ht[...])).astype(BF16)
         up[...] = (gs[...].astype(F32) + dot(qb[...], ft)).astype(BF16).reshape(nf, rows, width)
         lax.fori_loop(1, nf, send_up, 0)
-        s_r[block] = new[f]
+        s_r[block] = new[piece_of(f)]
         upd_out[block] = up[f]
         wait_bytes(s_r.at[pl.ds(0, count - 1)], out_sem.at[1])
 
@@ -288,39 +310,57 @@
     def _():
         wait_bytes(s_r, out_sem.at[1])
 
-    def scatter(i, carry):
-        t = lax.rem(f + i, nf)
+    for i in range(npiece - 1, 0, -1):
+        level, t = near(i, away(z))
         for q in (0, 1):
-            s_x[t, q] = s_r[back[2 * t + q]]
-        put(s_x.at[t], nk_out.at[:, f], out_sem.at[4], out_sem.at[5], (t, r))
-        return carry
-
-    lax.fori_loop(1, nf, scatter, 0)
+            s_x[i, q] = s_r[back[2 * t + q]]
+        put(s_x.at[i], nk_out.at[:, piece_of(f)], out_sem.at[4], out_sem.at[5], (t, r))
     for q in (0, 1):
-        nk_out[q, f] = s_r[back[2 * f + q]]
+        nk_out[q, piece_of(f)] = s_r[back[2 * f + q]]
 
     wait_bytes(rc, send_sem.at[0])
-    wait_bytes(sk_r.at[pl.ds(0, nf - 1)], send_sem.at[1])
+    wait_bytes(sk_r.at[pl.ds(0, npiece - 1)], send_sem.at[1])
     wait_bytes(s_a, send_sem.at[2])
     wait_bytes(s_b, send_sem.at[3])
     wait_bytes(ss_a.at[pl.ds(0, nr - 1)], send_sem.at[5])
     wait_bytes(ss_b.at[pl.ds(0, nf - 1)], send_sem.at[7])
-    wait_bytes(s_x.at[pl.ds(0, nf - 1)], out_sem.at[4])
-    wait_bytes(nk_out.at[:, pl.ds(0, nf - 1)], out_sem.at[5])
+    wait_bytes(s_x.at[pl.ds(0, npiece - 1)], out_sem.at[4])
+    wait_bytes(nk_out.at[:, pl.ds(0, npiece - 1)], out_sem.at[5])
 
     @pl.when(busy)
     def _():
         wait_bytes(g_out.at[pl.ds(0, count - 1)], send_sem.at[4])
-        wait_bytes(z_out.at[pl.ds(0, count - 1)], send_sem.at[6])
-        wait_bytes(new.at[pl.ds(0, nf - 1)], out_sem.at[0])
+        wait_bytes(z_one.at[pl.ds(0, count - 1)], send_sem.at[6])
+        wait_bytes(z_one.at[pl.ds(0, nf - 1)], out_sem.at[0])
         wait_bytes(up.at[pl.ds(0, nf - 1)], out_sem.at[2])
         wait_bytes(upd_out.at[pl.ds(0, count - 1)], out_sem.at[3])
 
     @pl.when(jnp.logical_not(busy))
     def _():
         wait_bytes(g_out.at[pl.ds(0, count)], send_sem.at[4])
-        wait_bytes(z_out.at[pl.ds(0, count)], send_sem.at[6])
+        wait_bytes(z_one.at[pl.ds(0, count)], send_sem.at[6])
         wait_bytes(upd_out, out_sem.at[3])
+
+
+def finish_kernel(count, table, upd, fresh, held, upd_out, sketch_out, sem):
+    first = pltpu.make_async_copy(upd, upd_out, sem.at[0])
+    first.start()
+    f = lax.axis_index("fsdp")
+    base = lax.axis_index("rep") * count
+    filled = sum(((table[base + j] == f).astype(jnp.int32) for j in range(count)), jnp.int32(0))
+    for q in (0, 1):
+
+        @pl.when(q < filled)
+        def _():
+            pltpu.make_async_copy(fresh.at[q], sketch_out.at[0, 0, q], sem.at[1 + q]).start()
+
+        @pl.when(q >= filled)
+        def _():
+            pltpu.make_async_copy(held.at[q], sketch_out.at[0, 0, q], sem.at[1 + q]).start()
+
+    first.wait()
+    for q in (0, 1):
+        pltpu.make_async_copy(fresh.at[q], sketch_out.at[0, 0, q], sem.at[1 + q]).wait()
 
 
 def local(nf, nr, partials, sketch, owner_table):
@@ -335,11 +375,12 @@
     dma = pltpu.SemaphoreType.DMA
     tall, wide = pltpu.VMEM((width, rank), BF16), pltpu.VMEM((rank, width), BF16)
     held = sketch[0, 0]
+    table = owner_table[:, 0]
     upd, fresh = pl.pallas_call(
         functools.partial(step_kernel, nf, nr, 0.5 * math.sqrt(blocks_all * width * width)),
         out_shape=(
             jax.ShapeDtypeStruct((per_slice, rows, width), BF16),
-            jax.ShapeDtypeStruct((2, nf, rows, rank), BF16),
+            jax.ShapeDtypeStruct((2, nf // 2, 2 * rows, rank), BF16),
         ),
         in_specs=[smem, anyw, anyw],
         out_specs=(vmem, vmem),
@@ -351,20 +392,21 @@
             pltpu.VMEM((2, 2, half, rows, width), BF16),
             pltpu.VMEM((2, 2, half, rows, width), BF16),
             pltpu.VMEM((2, half, rows, width), BF16),
-            pltpu.VMEM((nf, 2, rows, rank), BF16),
-            pltpu.VMEM((per_slice, rows, rank), BF16),
+            pltpu.VMEM((nf, 2, 2 * rows, rank), BF16),
+            pltpu.VMEM((per_slice, 2 * rows, rank), BF16),
             pltpu.VMEM((nr, 8, 128), F32),
             pltpu.VMEM((nf, 8, 128), F32),
             pltpu.VMEM((nf, rows, width), BF16),
-            pltpu.VMEM((nf, rows, rank), BF16),
+            pltpu.VMEM((2, nf // 2, 2 * rows, rank), BF16),
+            pltpu.VMEM((nf // 2, 2 * rows, rank), BF16),
             pltpu.VMEM((width, rank), F32),
             pltpu.VMEM((rank, width), F32),
             pltpu.VMEM((width, width), BF16),
             wide, wide, tall, tall, wide, wide, tall, wide, wide,
             pltpu.VMEM((nf, rows, width), BF16),
-            pltpu.VMEM((nf, rows, rank), BF16),
-            pltpu.VMEM((per_slice, rows, rank), BF16),
-            pltpu.VMEM((nf, 2, rows, rank), BF16),
+            pltpu.VMEM((nf // 2, 2 * rows, rank), BF16),
+            pltpu.VMEM((per_slice, 2 * rows, rank), BF16),
+            pltpu.VMEM((nf // 2, 2, 2 * rows, rank), BF16),
             pltpu.SMEM((per_slice,), jnp.int32),
             pltpu.SMEM((2 * nf,), jnp.int32),
             dma((ny,)),
@@ -375,13 +417,20 @@
             dma((8,)),
             dma((6,)),
         ],
-        compiler_params=pltpu.CompilerParams(collective_id=0, has_side_effects=True),
-    )(owner_table[:, 0], partials.reshape(nr, 2, half, rows, width), held)
-
-    owners = lax.dynamic_slice_in_dim(owner_table[:, 0], lax.axis_index("rep") * per_slice, per_slice)
-    filled = jnp.sum((owners == lax.axis_index("fsdp")).astype(jnp.int32))
-    keep = jnp.arange(2, dtype=jnp.int32)[:, None, None] < filled
-    return upd, jnp.where(keep, fresh.reshape(2, width, rank), held)[None, None]
+        compiler_params=pltpu.CompilerParams(collective_id=0, has_side_effects=True, vmem_limit_bytes=48 * 2**20),
+    )(table, partials.reshape(nr, 2, half, rows, width), held)
+
+    return pl.pallas_call(
+        functools.partial(finish_kernel, per_slice),
+        out_shape=(
+            jax.ShapeDtypeStruct((per_slice, rows, width), BF16),
+            jax.ShapeDtypeStruct((1, 1, 2, width, rank), BF16),
+        ),
+        in_specs=[smem, vmem, vmem, vmem],
+        out_specs=(anyw, anyw),
+        scratch_shapes=[dma((3,))],
+        compiler_params=pltpu.CompilerParams(vmem_limit_bytes=4 * 2**20),
+    )(table, upd, fresh.reshape(2, width, rank), held)
 
 
 def solution(mesh):

time: 140 us -> 130 us (0.929)
  Pallas kernels: 132 us -> 125 us
  other arithmetic: 4.47 us -> 0 us
    pallas_call x1, Pallas kernels: 132 us -> 124 us  [local(): pl.pallas_call(functools.partial(step_kernel, nf, nr, 0.5 * math.sqrt(blo...]
    select_n x1 -> x0, other arithmetic: 2.37 us -> none  [local(): jnp.where(keep, fresh.reshape(2, width, rank), held)[None, None]]
    pallas_call x0 -> x1, Pallas kernels: none -> 1.83 us  [local(): pl.pallas_call(functools.partial(finish_kernel, per_slice), out_shape=(ja...]
    reduce_sum x1 -> x0, other arithmetic: 1.45 us -> none  [local(): filled = jnp.sum((owners == lax.axis_index('fsdp')).astype(jnp.int32))]
where the time goes in v3:
time: 130 us; the launch traced here: 128 us
  Pallas kernels  125 us (96%)
  local copies, waits for them, and re-layouts  1.87 us (1%)
    pallas_call x1, Pallas kernels, local(): pl.pallas_call(functools.partial(step_kernel, nf, nr, 0.5 * math.sqrt(blo...  124 us

profile of v3, /device:TPU:2, one launch (start us, length us, event | category | flops | bytes accessed | tf_op | source)
XLA Modules:
  0.0 127.9 jit_solution(10423868933580251724)
XLA Ops:
  0.6 0.0 copy-start
  0.6 1.2 copy-done
  1.9 0.0 copy-start.1
  1.9 0.7 copy-done.1
  2.5 123.6 %shard_map.50 = (bf16[14,32,1024]{2,1,0:T(8,128)(2,1)S(1)}, bf16[2,16,64,256]{3,2,1,0:T(8,128)(2,1)S(1)}) custom-call(s32[112]{0:T(128)S(1)} %bitcast.7, bf16[8,2,7,32,1024]{4,3,2,1,0:T(8,128)(2,1)} %bitcast.9, bf16[2,1024,256]{2,1,0:T(8,128)(2,1)S(1)} %bitcast.4), custom_call_target="tpu_custom_call" | custom-call | tf_op jit(solution)/shard_map/pallas_call | solution.py:379
  126.1 1.8 %shard_map.51 = (bf16[14,32,1024]{2,1,0:T(8,128)(2,1)}, bf16[1,1,2,1024,256]{4,3,2,1,0:T(8,128)(2,1)}) custom-call(s32[112]{0:T(128)S(1)} %bitcast.8, bf16[14,32,1024]{2,1,0:T(8,128)(2,1)S(1)} %get-tuple-element.4.upd, bf16[2,1024,256]{2,1,0:T(8,128)(2,1)S(1)} %bitcast.6, bf16[2,1024,256]{2,1,0:T(8,128)(2,1)S(1)} %bitcast.5), custom_call_target="tpu_custom_call" | custom-call | tf_op jit(solution)/shard_map/pallas_call | solution.py:423
Async XLA Ops:
  0.6 1.2 copy-start
  1.9 0.7 copy-start.1

commit v4 on v3

--- a/solution.py
+++ b/solution.py
@@ -68,10 +68,10 @@
 
 
 def step_kernel(
-    nf, nr, limit, table, part, sk, upd_out, nk_out,
+    nf, nr, limit, table_in, part, sk, upd_out, nk_out,
     own, rc, s_a, r_a, s_b, r_b, fin, sk_r, sk_s, ss_a, ss_b, g_out, z_out, z_in, base, first,
-    gs, zt, at, wh, wl, wth, wtl, qb, qt, ht, up, new, s_r, s_x, slots, back,
-    own_sem, rc_sem, ra_sem, rb_sem, gz_sem, send_sem, out_sem,
+    gs, zt, at, wh, wl, wth, wtl, qb, qt, ht, up, new, s_r, s_x, slots, back, table,
+    tab_sem, own_sem, rc_sem, ra_sem, rb_sem, gz_sem, send_sem, out_sem,
 ):
     f = lax.axis_index("fsdp")
     r = lax.axis_index("rep")
@@ -96,6 +96,9 @@
     busy = (lax.rem(f + 5, 9) != 0) & (lax.rem(spot, 2) == c)
     block = spot // 2
 
+    owners_in = pltpu.make_async_copy(table_in, table, tab_sem.at[0])
+    owners_in.start()
+
     for d in (2, 1, 3, 0):
         pltpu.make_async_copy(part.at[2 * lax.rem(y + d, ny) + c], own.at[d], own_sem.at[d]).start()
 
@@ -129,6 +132,7 @@
         put(sk.at[:, cut(t), :], sk_r.at[f], send_sem.at[1], gz_sem.at[0], (t, r))
 
     count = 2 * steps
+    owners_in.wait()
     owners = [table[r * count + j] for j in range(count)]
     for j in range(count):
         slots[j] = 2 * owners[j] + sum(((owners[i] == owners[j]).astype(jnp.int32) for i in range(j)), jnp.int32(0))
@@ -216,7 +220,7 @@
             independent(order(i - 1))
         if 2 <= i < steps + 2:
             dependent(order(i - 2))
-        if i == steps + 1:
+        if i == 4:
             sketches()
         if i >= 3:
             total = final(order(i - 3), total)
@@ -371,6 +375,7 @@
     ny = nr // 2
     vmem = pl.BlockSpec(memory_space=pltpu.VMEM)
     anyw = pl.BlockSpec(memory_space=pl.ANY)
+    hbm = pl.BlockSpec(memory_space=pltpu.HBM)
     smem = pl.BlockSpec(memory_space=pltpu.SMEM)
     dma = pltpu.SemaphoreType.DMA
     tall, wide = pltpu.VMEM((width, rank), BF16), pltpu.VMEM((rank, width), BF16)
@@ -382,7 +387,7 @@
             jax.ShapeDtypeStruct((per_slice, rows, width), BF16),
             jax.ShapeDtypeStruct((2, nf // 2, 2 * rows, rank), BF16),
         ),
-        in_specs=[smem, anyw, anyw],
+        in_specs=[hbm, hbm, hbm],
         out_specs=(vmem, vmem),
         scratch_shapes=[
             pltpu.VMEM((ny, 2, half, rows, width), BF16),
@@ -409,6 +414,8 @@
             pltpu.VMEM((nf // 2, 2, 2 * rows, rank), BF16),
             pltpu.SMEM((per_slice,), jnp.int32),
             pltpu.SMEM((2 * nf,), jnp.int32),
+            pltpu.SMEM((blocks_all,), jnp.int32),
+            dma((1,)),
             dma((ny,)),
             dma((ny, half)),
             dma((2, half)),

time: 130 us -> 123 us (0.946); the launches traced: 128 us -> 123 us
  Pallas kernels: 125 us -> 120 us
    pallas_call x1, Pallas kernels: 124 us -> 118 us  [local(): pl.pallas_call(functools.partial(step_kernel, nf, nr, 0.5 * math.sqrt(blo...]
where the time goes in v4:
time: 123 us
  Pallas kernels  120 us (98%)
  local copies, waits for them, and re-layouts  1.87 us (2%)
    pallas_call x1, Pallas kernels, local(): pl.pallas_call(functools.partial(step_kernel, nf, nr, 0.5 * math.sqrt(blo...  118 us

profile of v4, /device:TPU:2, one launch (start us, length us, event | category | flops | bytes accessed | tf_op | source)
XLA Modules:
  0.0 122.7 jit_solution(17928390777456746394)
XLA Ops:
  0.6 0.0 copy-start
  0.6 1.2 copy-done
  1.9 0.0 copy-start.1
  1.9 0.7 copy-done.1
  2.5 118.4 %shard_map.50 = (bf16[14,32,1024]{2,1,0:T(8,128)(2,1)S(1)}, bf16[2,16,64,256]{3,2,1,0:T(8,128)(2,1)S(1)}) custom-call(s32[112]{0:T(128)S(1)} %bitcast.7, bf16[8,2,7,32,1024]{4,3,2,1,0:T(8,128)(2,1)} %bitcast.9, bf16[2,1024,256]{2,1,0:T(8,128)(2,1)S(1)} %bitcast.4), custom_call_target="tpu_custom_call" | custom-call | tf_op jit(solution)/shard_map/pallas_call | solution.py:384
  120.9 1.8 %shard_map.51 = (bf16[14,32,1024]{2,1,0:T(8,128)(2,1)}, bf16[1,1,2,1024,256]{4,3,2,1,0:T(8,128)(2,1)}) custom-call(s32[112]{0:T(128)S(1)} %bitcast.8, bf16[14,32,1024]{2,1,0:T(8,128)(2,1)S(1)} %get-tuple-element.4.upd, bf16[2,1024,256]{2,1,0:T(8,128)(2,1)S(1)} %bitcast.6, bf16[2,1024,256]{2,1,0:T(8,128)(2,1)S(1)} %bitcast.5), custom_call_target="tpu_custom_call" | custom-call | tf_op jit(solution)/shard_map/pallas_call | solution.py:430
Async XLA Ops:
  0.6 1.2 copy-start
  1.9 0.7 copy-start.1

commit v5 on v4

--- a/solution.py
+++ b/solution.py
@@ -99,6 +99,11 @@
     owners_in = pltpu.make_async_copy(table_in, table, tab_sem.at[0])
     owners_in.start()
 
+    def far_first(send):
+        hops = lambda o: min(o // nx, nz - o // nx) + min(o % nx, nx - o % nx)
+        for o in sorted(range(1, nf), key=lambda o: -hops(o)):
+            send(lax.rem(z + o // nx, nz) * nx + lax.rem(x + o % nx, nx))
+
     for d in (2, 1, 3, 0):
         pltpu.make_async_copy(part.at[2 * lax.rem(y + d, ny) + c], own.at[d], own_sem.at[d]).start()
 
@@ -213,17 +218,17 @@
                 z_out[f // npiece, piece_of(f)] = sk_s[j]
 
     total = jnp.zeros((8, 128), F32)
-    for i in range(steps + 3):
+    for i in range(steps + 2):
         if i < steps:
             opposite(order(i))
         if 1 <= i < steps + 1:
             independent(order(i - 1))
-        if 2 <= i < steps + 2:
-            dependent(order(i - 2))
+        if 1 <= i < steps + 1:
+            dependent(order(i - 1))
         if i == 4:
             sketches()
-        if i >= 3:
-            total = final(order(i - 3), total)
+        if i >= 2:
+            total = final(order(i - 2), total)
 
     ss_a[r] = total
 
@@ -291,21 +296,17 @@
         inner_part = dot(energy_h, inverse_h) + (dot(energy_h, inverse_l) + dot(energy_l, inverse_h))
         new[...] = dot(qb[...], inner_part.astype(BF16)).astype(BF16).reshape(npiece, prow, rank)
 
-        def send_new(i, carry):
-            t = lax.rem(f + i, nf)
+        def send_new(t):
             put(new.at[piece_of(t)], s_r.at[block], out_sem.at[0], out_sem.at[1], (t, r))
-            return carry
-
-        def send_up(i, carry):
-            t = lax.rem(f + i, nf)
+
+        def send_up(t):
             put(up.at[t], upd_out.at[block], out_sem.at[2], out_sem.at[3], (t, r))
-            return carry
-
-        lax.fori_loop(1, nf, send_new, 0)
+
+        far_first(send_new)
         mix_h, mix_l = split(math.sqrt(DAMPING) * inverse - eye)
         ft = (dot(mix_h, ht[...]) + dot(mix_l, ht[...])).astype(BF16)
         up[...] = (gs[...].astype(F32) + dot(qb[...], ft)).astype(BF16).reshape(nf, rows, width)
-        lax.fori_loop(1, nf, send_up, 0)
+        lax.fori_loop(1, nf, lambda i, carry: (send_up(lax.rem(f + i, nf)), carry)[1], 0)
         s_r[block] = new[piece_of(f)]
         upd_out[block] = up[f]
         wait_bytes(s_r.at[pl.ds(0, count - 1)], out_sem.at[1])
@@ -424,7 +425,7 @@
             dma((8,)),
             dma((6,)),
         ],
-        compiler_params=pltpu.CompilerParams(collective_id=0, has_side_effects=True, vmem_limit_bytes=48 * 2**20),
+        compiler_params=pltpu.CompilerParams(collective_id=0, has_side_effects=True, vmem_limit_bytes=52 * 2**20),
     )(table, partials.reshape(nr, 2, half, rows, width), held)
 
     return pl.pallas_call(

time: 123 us -> 120 us (0.976)
    pallas_call x1, Pallas kernels: 118 us -> 117 us  [local(): pl.pallas_call(functools.partial(step_kernel, nf, nr, 0.5 * math.sqrt(blo...]
where the time goes in v5:
time: 120 us
  Pallas kernels  119 us (99%)
    pallas_call x1, Pallas kernels, local(): pl.pallas_call(functools.partial(step_kernel, nf, nr, 0.5 * math.sqrt(blo...  117 us

profile of v5, /device:TPU:2, one launch (start us, length us, event | category | flops | bytes accessed | tf_op | source)
XLA Modules:
  0.0 120.3 jit_solution(3355270745614492354)
XLA Ops:
  0.6 0.0 copy-start
  0.6 0.0 copy-start.1
  0.6 0.7 copy-done.1
  1.4 117.0 %shard_map.50 = (bf16[14,32,1024]{2,1,0:T(8,128)(2,1)S(1)}, bf16[2,16,64,256]{3,2,1,0:T(8,128)(2,1)S(1)}) custom-call(s32[112]{0:T(128)S(1)} %bitcast.7, bf16[8,2,7,32,1024]{4,3,2,1,0:T(8,128)(2,1)} %bitcast.9, bf16[2,1024,256]{2,1,0:T(8,128)(2,1)} %bitcast.4), custom_call_target="tpu_custom_call" | custom-call | tf_op jit(solution)/shard_map/pallas_call | solution.py:385
  118.4 0.0 copy-done
  118.5 1.8 %shard_map.51 = (bf16[14,32,1024]{2,1,0:T(8,128)(2,1)}, bf16[1,1,2,1024,256]{4,3,2,1,0:T(8,128)(2,1)}) custom-call(s32[112]{0:T(128)S(1)} %bitcast.8, bf16[14,32,1024]{2,1,0:T(8,128)(2,1)S(1)} %get-tuple-element.4.upd, bf16[2,1024,256]{2,1,0:T(8,128)(2,1)S(1)} %bitcast.6, bf16[2,1024,256]{2,1,0:T(8,128)(2,1)S(1)} %bitcast.5), custom_call_target="tpu_custom_call" | custom-call | tf_op jit(solution)/shard_map/pallas_call | solution.py:431
Async XLA Ops:
  0.6 117.8 %copy-start = (bf16[1,1,2,1024,256]{4,3,2,1,0:T(8,128)(2,1)S(1)}, bf16[1,1,2,1024,256]{4,3,2,1,0:T(8,128)(2,1)}, u32[]{:S(2)}) copy-start(bf16[1,1,2,1024,256]{4,3,2,1,0:T(8,128)(2,1)} %param.4) | copy-start | bytes 3145732
  0.6 0.7 copy-start.1
